TPU v7x, 32 devices: a whole 2x2x4 slice. The times are simulated.
32 devices in a mesh: seq: 2 (over x), dp: 16 (over z, y, core).
Axes of the slice: x: 2, y: 2, z: 4, core: 2. Of those that a mesh axis runs over, the one named last changes fastest.
Arguments:
- accept_arrays: bfloat16 [16, 256, 2048], P('dp', 'seq'), may hold values from -1.5 to 1.5
- lookup_arrays: bfloat16 [16, 256, 2048], P('dp', 'seq'), may hold values from -0.75 to 0.75
- payload_arrays: bfloat16 [16, 256, 2048], P('dp', 'seq'), may hold values from -6 to 6
- fading_exponent: bfloat16 [16, 256, 2048], P('dp', 'seq'), may hold values from -14 to 1
- self_boost: float32 [32, 64], replicated, may hold values from -3 to 3
- result_cotangent: bfloat16 [16, 256, 2048], P('dp', 'seq'), may hold values from -0.75 to 0.75
- initial_memory_matrix: float32 [2048, 64], replicated, may hold values from -12 to 12
Outputs:
- receptance_grad: bfloat16 [16, 256, 2048], P('dp', 'seq')
- lookup_cotangent: bfloat16 [16, 256, 2048], P('dp', 'seq')
- value_grad: bfloat16 [16, 256, 2048], P('dp', 'seq')
- state_grad: float32 [2048, 64], P('dp', 'seq')
All inputs are finite; a program needn't handle non-finite values.
Results may differ from a plain program's by a relative error of at most 0.001.
Values sent between devices are 32-bit elements; how exact they have to be, the bound alone decides.
No kernel may reach another device: no remote copies, remote signals or barrier semaphores. Data moves between devices by JAX's collectives and lax.ppermute only.
A program may use at most 128 MiB of HBM per device.

v0:
```python
import jax
import jax.numpy as jnp
from jax import lax
from jax.experimental import pallas as pl
from jax.experimental.pallas import tpu as pltpu
from jax.sharding import PartitionSpec as P

LANES = 128
CHUNK = 32
BF16 = jnp.bfloat16
F32 = jnp.float32


def dot(a, b, contract=(1, 0)):
    return lax.dot_general(
        a, b, (((contract[0],), (contract[1],)), ((), ())), preferred_element_type=F32
    )


def split(x):
    hi = x.astype(BF16)
    return hi, (x - hi.astype(F32)).astype(BF16)


def triangles(toks):
    row = lax.broadcasted_iota(jnp.int32, (toks, toks), 0)
    col = lax.broadcasted_iota(jnp.int32, (toks, toks), 1)
    same = (row // CHUNK) == (col // CHUNK)
    before = jnp.where(same & (col < row), 1.0, 0.0).astype(BF16)
    after = jnp.where(same & (col > row), 1.0, 0.0).astype(BF16)
    return jnp.concatenate([before, after], 0)


def decays(fade, tri):
    toks = fade.shape[0]
    log_decay = -jnp.exp(fade.astype(F32))
    hi, lo = split(log_decay)
    sums = dot(jnp.concatenate([tri, tri], 1), jnp.concatenate([hi, lo], 0))
    prefix, suffix = sums[:toks], sums[toks:]
    totals, middles = [], []
    for c in range(toks // CHUNK):
        last = (c + 1) * CHUNK - 1
        totals.append(prefix[last : last + 1] + log_decay[last : last + 1])
        mid = c * CHUNK + CHUNK // 2
        middles.append(prefix[mid : mid + 1])
    return jnp.exp(prefix), jnp.exp(suffix), totals, middles


def spread(early, late, totals):
    chunks = len(totals)
    rows = [slice(c * CHUNK, (c + 1) * CHUNK) for c in range(chunks)]
    from_start, to_end = [], []
    run = jnp.zeros_like(totals[0])
    for c in range(chunks):
        from_start.append(early[rows[c]] * jnp.exp(run))
        run = run + totals[c]
    whole = jnp.exp(run)
    run = jnp.zeros_like(totals[0])
    for c in reversed(range(chunks)):
        to_end.append(late[rows[c]] * jnp.exp(run))
        run = run + totals[c]
    return jnp.concatenate(from_start, 0), jnp.concatenate(to_end[::-1], 0), whole


def first_head(shape):
    return lax.broadcasted_iota(jnp.int32, shape, len(shape) - 1) < (LANES // 2)


def by_head(x):
    keep = first_head(x.shape)
    zero = jnp.zeros_like(x)
    return jnp.concatenate([jnp.where(keep, x, zero), jnp.where(keep, zero, x)], 0)


def diagonal(x):
    half = x.shape[0] // 2
    return jnp.where(first_head((half, LANES)), x[:half], x[half:])


def state_kernel(pairs, fast, flag, r, k, v, f, dy, init, *outs):
    toks = r.shape[0]
    tri = triangles(toks)
    step = pl.program_id(0)
    for p in range(pairs):
        at = slice(p * LANES, (p + 1) * LANES)
        early, late, totals, _ = decays(f[:, at], tri)
        from_start, to_end, whole = spread(early, late, totals)
        key_hi, key_lo = split(k[:, at].astype(F32) * to_end)
        rec_hi, rec_lo = split(r[:, at].astype(F32) * from_start)
        state = dot(v[:, at], jnp.concatenate([key_hi, key_lo], 1), (0, 0))
        grad = dot(dy[:, at], jnp.concatenate([rec_hi, rec_lo], 1), (0, 0))
        state = diagonal(state[:, :LANES] + state[:, LANES:])
        grad = diagonal(grad[:, :LANES] + grad[:, LANES:])
        if fast:
            sent, kept, swapped = outs
            half = grad.shape[0] // 2
            is_first = flag[0] == 0
            end = whole * init[:, at] + state
            swapped[p] = jnp.where(is_first, end, grad)
            pair = step * pairs + p
            sent[pair] = jnp.where(is_first, grad[half:], grad[:half])
            kept[p] = jnp.where(is_first, grad[:half], grad[half:])
            sent[sent.shape[0] - 1, pl.ds(pair, 1), :] = whole
        else:
            states, grads, wholes = outs
            states[p] = state
            grads[p] = grad
            wholes[p] = whole


def inner_kernel(pairs, r, k, v, f, dy, boost, rec, key, val, from_out, to_out):
    toks = r.shape[0]
    chunks = toks // CHUNK
    tri = triangles(toks)
    keep = first_head((toks, LANES))
    keep_chunk = first_head((CHUNK, LANES))
    row = lax.broadcasted_iota(jnp.int32, (CHUNK, CHUNK), 0)
    col = lax.broadcasted_iota(jnp.int32, (CHUNK, CHUNK), 1)
    wide_row = lax.broadcasted_iota(jnp.int32, (toks, toks), 0)
    wide_col = lax.broadcasted_iota(jnp.int32, (toks, toks), 1)
    below = wide_col < wide_row
    reversed_tok = (chunks - 1 - wide_col // CHUNK) * CHUNK + wide_col % CHUNK
    above = reversed_tok > wide_row

    def flip(x):
        return jnp.concatenate(
            [x[c * CHUNK : (c + 1) * CHUNK] for c in reversed(range(chunks))], 0
        )

    rows = [slice(c * CHUNK, (c + 1) * CHUNK) for c in range(chunks)]
    for p in range(pairs):
        at = slice(p * LANES, (p + 1) * LANES)
        early, late, totals, middles = decays(f[:, at], tri)
        from_start, to_end, _ = spread(early, late, totals)
        from_out[:, at] = from_start
        to_out[:, at] = to_end
        rb, kb, vb, db = r[:, at], k[:, at], v[:, at], dy[:, at]
        rf, kf, vf, df = (x.astype(F32) for x in (rb, kb, vb, db))
        u = boost[:, at]
        rec_early = rf * early
        key_late = kf * late
        dy_heads = by_head(flip(db))
        scores = dot(db, by_head(vb), (1, 1))
        scores_t = dot(vb, dy_heads, (1, 1))
        scores_split, scores_t_split = [], []
        for h in range(2):
            part = slice(h * toks, (h + 1) * toks)
            scores_split.append(split(jnp.where(below, scores[:, part], 0.0)))
            scores_t_split.append(split(jnp.where(above, scores_t[:, part], 0.0)))
        rec_rows, key_rows, cross_rows = [], [], []
        for c in range(chunks):
            here = rows[c]
            count = (c + 1) * CHUNK
            pieces = [key_late[here] * jnp.exp(middles[c] - totals[c])]
            gap = middles[c]
            for e in reversed(range(c)):
                pieces.append(key_late[rows[e]] * jnp.exp(gap))
                gap = gap + totals[e]
            key_hi, key_lo = split(jnp.concatenate(pieces[::-1], 0))
            stack = jnp.concatenate(
                [s[i][here, :count] for i in range(2) for s in scores_split], 0
            )
            got = dot(stack, jnp.concatenate([key_hi, key_lo], 1))
            got = got[:, :LANES] + got[:, LANES:]
            got = got[: 2 * CHUNK] + got[2 * CHUNK :]
            got = jnp.where(keep_chunk, got[:CHUNK], got[CHUNK:])
            rec_rows.append(early[here] * jnp.exp(-middles[c]) * got)
            pieces = [rec_early[here] * jnp.exp(-middles[c])]
            gap = totals[c] - middles[c]
            for e in range(c + 1, chunks):
                pieces.append(rec_early[rows[e]] * jnp.exp(gap))
                gap = gap + totals[e]
            rec_hi, rec_lo = split(jnp.concatenate(pieces[::-1], 0))
            count = (chunks - c) * CHUNK
            stack = jnp.concatenate(
                [s[i][here, :count] for i in range(2) for s in scores_t_split], 0
            )
            got = dot(stack, jnp.concatenate([rec_hi, rec_lo], 1))
            got = got[:, :LANES] + got[:, LANES:]
            got = got[: 2 * CHUNK] + got[2 * CHUNK :]
            got = jnp.where(keep_chunk, got[:CHUNK], got[CHUNK:])
            key_rows.append(late[here] * jnp.exp(middles[c] - totals[c]) * got)
            own = slice(c * CHUNK, (c + 1) * CHUNK)
            lhs = jnp.concatenate([by_head(key_hi[own]), by_head(key_lo[own])], 0)
            if c:
                pad = jnp.zeros((c * CHUNK, LANES), BF16)
                rhs = jnp.concatenate([rec_hi, pad, rec_lo, pad], 0)
            else:
                rhs = jnp.concatenate([rec_hi, rec_lo], 0)
            got = dot(lhs, rhs, (1, 1))
            got = got[:, :toks] + got[:, toks:]
            got = got[: 2 * CHUNK] + got[2 * CHUNK :]
            cross_rows.append(
                [jnp.where(above[here], got[h * CHUNK : (h + 1) * CHUNK], 0.0) for h in range(2)]
            )
        cross = jnp.concatenate(
            [jnp.concatenate([c[h] for c in cross_rows], 0) for h in range(2)], 1
        )
        cross_hi, cross_lo = split(cross)
        inner_val = dot(cross_hi, dy_heads) + dot(cross_lo, dy_heads)
        prod = vf * df
        mix = rf * u * kf

        def head_sum(x):
            one = jnp.sum(jnp.where(keep, x, 0.0), axis=-1, keepdims=True)
            two = jnp.sum(jnp.where(keep, 0.0, x), axis=-1, keepdims=True)
            return jnp.where(keep, one, two)

        boosted = u * head_sum(prod)
        rec[:, at] = jnp.concatenate(rec_rows, 0) + kf * boosted
        key[:, at] = jnp.concatenate(key_rows, 0) + rf * boosted
        val[:, at] = inner_val + head_sum(mix) * df


def outer_kernel(
    pairs, fast, flag, k, v, dy, from_start, to_end, rec, key, val, init, state, grad, *outs
):
    rec_out, key_out, val_out = outs
    for p in range(pairs):
        at = slice(p * LANES, (p + 1) * LANES)
        if fast:
            is_first = flag[0] == 0
            got = state[p]
            start = jnp.where(is_first, init[:, at], got)
            after = jnp.where(is_first, got, 0.0)
        else:
            start = state[p]
            after = grad[p]
        start_hi, start_lo = split(by_head(start))
        after_hi, after_lo = split(by_head(after))
        db, vb = dy[:, at], v[:, at]
        from_state = dot(
            jnp.concatenate([db, db], 1), jnp.concatenate([start_hi, start_lo], 0)
        )
        rec_out[:, at] = (rec[:, at] + from_start[:, at] * from_state).astype(BF16)
        from_grad = dot(jnp.concatenate([vb, vb], 1), jnp.concatenate([after_hi, after_lo], 0))
        tail = to_end[:, at]
        key_out[:, at] = (key[:, at] + tail * from_grad).astype(BF16)
        key_hi, key_lo = split(k[:, at].astype(F32) * tail)
        wide = dot(key_hi, jnp.concatenate([after_hi, after_lo], 0), (1, 1))
        from_key = wide[:, :LANES] + wide[:, LANES:] + dot(key_lo, after_hi, (1, 1))
        val_out[:, at] = (val[:, at] + from_key).astype(BF16)


def on_device(seq_size, dp_size, r, k, v, f, boost, dy, init):
    batch, toks, width = r.shape
    heads, feature = boost.shape
    pairs = width // LANES
    group = 4 if pairs % 4 == 0 else 1
    grid = (pairs // group,)
    half = feature // 2
    block = group * LANES
    fast = (
        batch == 1
        and seq_size == 2
        and dp_size & (dp_size - 1) == 0
        and pairs % dp_size == 0
        and pairs <= half
    )
    seq = lax.axis_index("seq")
    is_first = seq == 0
    flag = jnp.reshape(seq, (1,)).astype(jnp.int32)
    boost_row = boost.reshape(1, width)
    init_t = init.T

    rows = pl.BlockSpec((toks, block), lambda i: (0, i))
    wide = pl.BlockSpec((feature, block), lambda i: (0, i))
    per_pair = pl.BlockSpec((group, feature, LANES), lambda i: (i, 0, 0))
    half_pair = pl.BlockSpec((group, half, LANES), lambda i: (i, 0, 0))
    scalar = pl.BlockSpec(memory_space=pltpu.SMEM)
    params = pltpu.CompilerParams(
        dimension_semantics=("arbitrary",), vmem_limit_bytes=24 * 2**20
    )

    def like(shape, kind=F32):
        return jax.ShapeDtypeStruct(shape, kind)

    def states(b):
        if fast:
            shapes = (
                like((pairs + 1, half, LANES)),
                like((pairs, half, LANES)),
                like((pairs, feature, LANES)),
            )
            specs = (
                pl.BlockSpec((pairs + 1, half, LANES), lambda i: (0, 0, 0)),
                half_pair,
                per_pair,
            )
        else:
            shapes = (
                like((pairs, feature, LANES)),
                like((pairs, feature, LANES)),
                like((pairs, 1, LANES)),
            )
            specs = (per_pair, per_pair, pl.BlockSpec((group, 1, LANES), lambda i: (i, 0, 0)))

        def body(*refs):
            state_kernel(group, fast, *refs)

        return pl.pallas_call(
            body,
            grid=grid,
            in_specs=[scalar] + [rows] * 5 + [wide],
            out_specs=specs,
            out_shape=shapes,
            compiler_params=params,
            name="states",
            cost_estimate=pl.CostEstimate(
                flops=4 * 10**9, bytes_accessed=4 * 2**20, transcendentals=10**6
            ),
        )(flag, r[b], k[b], v[b], f[b], dy[b], init_t)

    def inner(b):
        def body(*refs):
            inner_kernel(group, *refs)

        return pl.pallas_call(
            body,
            grid=grid,
            in_specs=[rows] * 5 + [pl.BlockSpec((1, block), lambda i: (0, i))],
            out_specs=(rows,) * 5,
            out_shape=(like((toks, width)),) * 5,
            compiler_params=params,
            name="inner",
            cost_estimate=pl.CostEstimate(
                flops=10**10, bytes_accessed=8 * 2**20, transcendentals=10**6
            ),
        )(r[b], k[b], v[b], f[b], dy[b], boost_row)

    def outer(b, partial, state, grad):
        rec, key, val, from_start, to_end = partial

        def body(*refs):
            outer_kernel(group, fast, *refs)

        return pl.pallas_call(
            body,
            grid=grid,
            in_specs=[scalar] + [rows] * 8 + [wide, per_pair, per_pair],
            out_specs=(rows,) * 3,
            out_shape=(like((toks, width), BF16),) * 3,
            compiler_params=params,
            name="outer",
            cost_estimate=pl.CostEstimate(
                flops=3 * 10**9, bytes_accessed=9 * 2**20, transcendentals=0
            ),
        )(flag, k[b], v[b], dy[b], from_start, to_end, rec, key, val, init_t, state, grad)

    if fast:
        sent, kept, swapped = states(0)
        swap = [(0, 1), (1, 0)]
        got = lax.ppermute(sent, "seq", swap)
        other = lax.ppermute(swapped, "seq", swap)
        partial = inner(0)
        whole = jnp.where(is_first, sent[pairs, :pairs], got[pairs, :pairs])[:, None, :]
        total = jnp.where(is_first, kept, got[:pairs]) + whole * jnp.where(
            is_first, got[:pairs], kept
        )
        place = lax.axis_index("dp")
        total = total.reshape(dp_size, pairs // dp_size, half, LANES)
        bit = 1
        while bit < dp_size:
            couples = total.reshape((total.shape[0] // 2, 2) + total.shape[1:])
            upper = (place & bit) != 0
            mine = jnp.where(upper, couples[:, 1], couples[:, 0])
            theirs = jnp.where(upper, couples[:, 0], couples[:, 1])
            total = mine + lax.ppermute(
                theirs, "dp", [(i, i ^ bit) for i in range(dp_size)]
            )
            bit *= 2
        state_grad = total[0].transpose(0, 2, 1).reshape(-1, half)
        rec, key, val = outer(0, partial, other, other)
        return rec[None], key[None], val[None], state_grad

    forward = [(i, i + 1) for i in range(seq_size - 1)]
    backward = [(i + 1, i) for i in range(seq_size - 1)]
    start_t = init_t.reshape(feature, pairs, LANES).transpose(1, 0, 2)
    results, term = [], 0.0
    for b in range(batch):
        state_local, grad_local, whole = states(b)
        start = start_t
        after = jnp.zeros_like(grad_local)
        for _ in range(seq_size - 1):
            end = whole * start + state_local
            start = jnp.where(is_first, start_t, lax.ppermute(end, "seq", forward))
            after = lax.ppermute(grad_local + whole * after, "seq", backward)
        results.append(outer(b, inner(b), start, after))
        term = term + jnp.where(is_first, grad_local + whole * after, 0.0)
    term = term.transpose(0, 2, 1).reshape(width, feature)
    summed = lax.psum_scatter(term, "dp", scatter_dimension=0, tiled=True)
    summed = lax.psum(summed, "seq")
    columns = feature // seq_size
    state_grad = lax.dynamic_slice_in_dim(summed, seq * columns, columns, 1)
    rec, key, val = (jnp.stack(x) for x in zip(*results))
    return rec, key, val, state_grad


def solution(mesh):
    sizes = dict(mesh.shape)
    rows = P("dp", "seq", None)

    def run(*args):
        return on_device(sizes["seq"], sizes["dp"], *args)

    return jax.shard_map(
        run,
        mesh=mesh,
        in_specs=(rows, rows, rows, rows, P(), rows, P()),
        out_specs=(rows, rows, rows, P("dp", "seq")),
        check_vma=False,
    )
```

profile of v0, /device:TPU:0, one launch (start us, length us, event | category | flops | bytes accessed | tf_op | source)
XLA Modules:
  0.0 49.2 jit_solution(3603344384515065310)
XLA Ops:
  0.6 0.0 copy-start
  0.6 1.0 %copy-done = bf16[1,128,2048]{2,1,0:T(8,128)(2,1)S(1)} copy-done((bf16[1,128,2048]{2,1,0:T(8,128)(2,1)S(1)}, bf16[1,128,2048]{2,1,0:T(8,128)(2,1)}, u32[]{:S(2)}) %copy-start) | copy-done | bytes 524312
  1.7 0.0 copy-start.2
  1.7 1.0 %copy-done.2 = bf16[1,128,2048]{2,1,0:T(8,128)(2,1)S(1)} copy-done((bf16[1,128,2048]{2,1,0:T(8,128)(2,1)S(1)}, bf16[1,128,2048]{2,1,0:T(8,128)(2,1)}, u32[]{:S(2)}) %copy-start.2) | copy-done | bytes 524312
  2.7 0.0 copy-start.4
  2.7 1.0 %copy-done.4 = bf16[1,128,2048]{2,1,0:T(8,128)(2,1)S(1)} copy-done((bf16[1,128,2048]{2,1,0:T(8,128)(2,1)S(1)}, bf16[1,128,2048]{2,1,0:T(8,128)(2,1)}, u32[]{:S(2)}) %copy-start.4) | copy-done | bytes 524312
  3.8 0.0 copy-start.6
  3.8 1.0 %copy-done.6 = bf16[1,128,2048]{2,1,0:T(8,128)(2,1)S(1)} copy-done((bf16[1,128,2048]{2,1,0:T(8,128)(2,1)S(1)}, bf16[1,128,2048]{2,1,0:T(8,128)(2,1)}, u32[]{:S(2)}) %copy-start.6) | copy-done | bytes 524312
  4.8 0.0 copy-start.8
  4.8 1.0 %copy-done.8 = bf16[1,128,2048]{2,1,0:T(8,128)(2,1)S(1)} copy-done((bf16[1,128,2048]{2,1,0:T(8,128)(2,1)S(1)}, bf16[1,128,2048]{2,1,0:T(8,128)(2,1)}, u32[]{:S(2)}) %copy-start.8) | copy-done | bytes 524312
  5.8 0.0 copy-start.10
  5.9 1.0 %copy-done.10 = f32[2048,64]{0,1:T(8,128)S(1)} copy-done((f32[2048,64]{0,1:T(8,128)S(1)}, f32[2048,64]{0,1:T(8,128)}, u32[]{:S(2)}) %copy-start.10) | copy-done | bytes 524312
  6.9 0.0 copy-start.9
  6.9 2.8 %states.1 = (f32[17,32,128]{2,1,0:T(8,128)S(1)}, f32[16,32,128]{2,1,0:T(8,128)S(1)}, f32[16,64,128]{2,1,0:T(8,128)S(1)}) custom-call(s32[1]{0:T(128)} %bitcast.refs_0_, bf16[128,2048]{1,0:T(8,128)(2,1)S(1)} %bitcast.91, bf16[128,2048]{1,0:T(8,128)(2,1)S(1)} %bitcast.95, bf16[128,2048]{1,0:T(8,128)(2,1)S(1)} %bitcast.98, bf16[128,2048]{1,0:T(8,128)(2,1)S(1)} %bitcast.93, ...), custom_call_target="tpu_custom_call" | custom-call | flops 4000000000 | bytes 4194304 | tf_op jit(solution)/shard_map/states/pallas_call | solution.py:301
  9.7 3.0 %collective-permute-start.1 = (f32[17,32,128]{2,1,0:T(8,128)S(1)}, f32[17,32,128]{2,1,0:T(8,128)S(1)}, u32[]{:S(2)}, u32[]{:S(2)}) collective-permute-start(f32[17,32,128]{2,1,0:T(8,128)S(1)} %get-tuple-element.25), channel_id=1, source_target_pairs={{0,16},{16,0},{1,17},{17,1},{2,18},{18,2},{3,19},{19,3},{4,20},{20... | collective-permute-start | bytes 835592 | tf_op jit(solution)/shard_map/ppermute | solution.py:353
  12.7 6.7 %collective-permute-done.1 = f32[17,32,128]{2,1,0:T(8,128)S(1)} collective-permute-done((f32[17,32,128]{2,1,0:T(8,128)S(1)}, f32[17,32,128]{2,1,0:T(8,128)S(1)}, u32[]{:S(2)}, u32[]{:S(2)}) %collective-permute-start.1) | collective-permute-done | bytes 278560 | tf_op jit(solution)/shard_map/ppermute | solution.py:353
  19.4 0.0 copy-start.7
  19.4 0.1 multiply_add_fusion
  19.4 0.0 copy-start.12
  19.4 0.0 copy-start.5
  19.5 0.1 collective-permute-start.2
  19.6 0.0 copy-start.1
  19.6 0.0 copy-start.3
  19.6 1.4 %collective-permute-done.2 = f32[8,1,32,128]{3,2,0,1:T(8,128)} collective-permute-done((f32[8,1,32,128]{3,2,0,1:T(8,128)S(1)}, f32[8,1,32,128]{3,2,0,1:T(8,128)}, u32[]{:S(2)}, u32[]{:S(2)}) %collective-permute-start.2) | collective-permute-done | bytes 131104 | tf_op jit(solution)/shard_map/ppermute | solution.py:368
  21.0 0.9 %bitcast_add_fusion = f32[8,1,32,128]{3,2,0,1:T(8,128)S(1)} fusion(f32[8,1,32,128]{3,2,0,1:T(8,128)} %collective-permute-done.2, f32[8,2,1,32,128]{4,3,1,0,2:T(8,128)S(1)} %bitcast.107, pred[]{:T(512)S(6)} %ne.15), kind=kLoop, calls=%fused_computation.3 | loop fusion | flops 65536 | bytes 524289 | tf_op jit(solution)/shard_map/add | solution.py:368
  22.0 1.8 %collective-permute-start.3 = (f32[4,1,32,128]{3,2,0,1:T(8,128)S(1)}, f32[4,1,32,128]{3,2,0,1:T(8,128)S(1)}, u32[]{:S(2)}, u32[]{:S(2)}) collective-permute-start(f32[4,1,32,128]{3,2,0,1:T(8,128)S(1)} %select_bitcast_fusion.1), channel_id=1, source_target_pairs={{0,2},{1,3},{2,0},{3,1},{4,6},{5,7},{6,4},{7,5},{8,10},{9,11},{10,... | collective-permute-start | bytes 196616 | tf_op jit(solution)/shard_map/ppermute | solution.py:368
  23.8 2.5 %collective-permute-done.3 = f32[4,1,32,128]{3,2,0,1:T(8,128)S(1)} collective-permute-done((f32[4,1,32,128]{3,2,0,1:T(8,128)S(1)}, f32[4,1,32,128]{3,2,0,1:T(8,128)S(1)}, u32[]{:S(2)}, u32[]{:S(2)}) %collective-permute-start.3) | collective-permute-done | bytes 65568 | tf_op jit(solution)/shard_map/ppermute | solution.py:368
  26.4 1.9 %collective-permute-start.4 = (f32[2,1,32,128]{3,2,0,1:T(8,128)S(1)}, f32[2,1,32,128]{3,2,0,1:T(8,128)S(1)}, u32[]{:S(2)}, u32[]{:S(2)}) collective-permute-start(f32[2,1,32,128]{3,2,0,1:T(8,128)S(1)} %select_bitcast_fusion.2), channel_id=1, source_target_pairs={{0,4},{1,5},{2,6},{3,7},{4,0},{5,1},{6,2},{7,3},{8,12},{9,13},{10,... | collective-permute-start | bytes 98312 | tf_op jit(solution)/shard_map/ppermute | solution.py:368
  28.2 1.5 %collective-permute-start = (f32[16,64,128]{2,1,0:T(8,128)S(1)}, f32[16,64,128]{2,1,0:T(8,128)}, u32[]{:S(2)}, u32[]{:S(2)}) collective-permute-start(f32[16,64,128]{2,1,0:T(8,128)S(1)} %get-tuple-element.20), channel_id=1, source_target_pairs={{0,16},{16,0},{1,17},{17,1},{2,18},{18,2},{3,19},{19,3},{4,20},{20... | collective-permute-start | bytes 1572872 | tf_op jit(solution)/shard_map/ppermute | solution.py:354
  29.7 0.0 copy-done.12
  29.7 0.1 reshape.214.refs_5_
  29.8 0.5 %collective-permute-done.4 = f32[2,1,32,128]{3,2,0,1:T(8,128)S(1)} collective-permute-done((f32[2,1,32,128]{3,2,0,1:T(8,128)S(1)}, f32[2,1,32,128]{3,2,0,1:T(8,128)S(1)}, u32[]{:S(2)}, u32[]{:S(2)}) %collective-permute-start.4) | collective-permute-done | bytes 32800 | tf_op jit(solution)/shard_map/ppermute | solution.py:368
  30.4 0.0 copy-start.11
  30.4 2.9 %collective-permute-start.5 = (f32[1,1,32,128]{3,2,1,0:T(8,128)S(1)}, f32[1,1,32,128]{3,2,1,0:T(8,128)S(1)}, u32[]{:S(2)}, u32[]{:S(2)}) collective-permute-start(f32[1,1,32,128]{3,2,1,0:T(8,128)S(1)} %fusion.4), channel_id=1, source_target_pairs={{0,8},{1,9},{2,10},{3,11},{4,12},{5,13},{6,14},{7,15},{8,0},{9,1},... | collective-permute-start | bytes 49160 | tf_op jit(solution)/shard_map/ppermute | solution.py:368
  33.3 0.0 copy-done.9
  33.3 0.0 copy-done.7
  33.3 0.0 copy-done.5
  33.3 0.0 copy-done.1
  33.3 0.0 copy-done.3
  33.3 10.7 %inner.1 = (f32[128,2048]{1,0:T(8,128)S(1)}, f32[128,2048]{1,0:T(8,128)S(1)}, f32[128,2048]{1,0:T(8,128)S(1)}, f32[128,2048]{1,0:T(8,128)S(1)}, f32[128,2048]{1,0:T(8,128)S(1)}) custom-call(bf16[128,2048]{1,0:T(8,128)(2,1)S(1)} %bitcast.92, bf16[128,2048]{1,0:T(8,128)(2,1)S(1)} %bitcast.96, bf16[128,2048]{1,0:T(8,128)(2,1)S(1)} %bitcast.99, ...), custom_call_target="tpu_custom_call" | custom-call | flops 10000000000 | bytes 8388608 | tf_op jit(solution)/shard_map/inner/pallas_call | solution.py:318
  44.0 0.0 collective-permute-done.5
  44.0 0.6 %fusion.5 = f32[128,32]{0,1:T(8,128)} fusion(f32[1,1,32,128]{3,2,1,0:T(8,128)S(1)} %collective-permute-done.5, f32[1,2,1,32,128]{4,3,1,2,0:T(8,128)S(1)} %bitcast.114, f32[1,2,1,32,128]{4,3,2,1,0:T(8,128)S(1)} %bitcast.115, pred[]{:T(512)S(6)} %ne.12), kind=kLoop, calls=%fused_computation.16 | loop fusion | flops 8192 | bytes 65537 | tf_op jit(solution)/shard_map/reshape | solution.py:372
  44.6 0.0 collective-permute-done.refs_10_.refs_11_
  44.7 0.0 copy-done.11
  44.7 4.6 %outer.1 = (bf16[128,2048]{1,0:T(8,128)(2,1)}, bf16[128,2048]{1,0:T(8,128)(2,1)}, bf16[128,2048]{1,0:T(8,128)(2,1)}) custom-call(s32[1]{0:T(128)} %bitcast.refs_0_, bf16[128,2048]{1,0:T(8,128)(2,1)S(1)} %bitcast.97, bf16[128,2048]{1,0:T(8,128)(2,1)S(1)} %bitcast.100, bf16[128,2048]{1,0:T(8,128)(2,1)S(1)} %bitcast.103, ...), custom_call_target="tpu_custom_call" | custom-call | flops 3000000000 | bytes 9437184 | tf_op jit(solution)/shard_map/outer/pallas_call | solution.py:337
  (7 shorter events, 0.1 us)
Async XLA Ops:
  0.6 1.0 %copy-start = (bf16[1,128,2048]{2,1,0:T(8,128)(2,1)S(1)}, bf16[1,128,2048]{2,1,0:T(8,128)(2,1)}, u32[]{:S(2)}) copy-start(bf16[1,128,2048]{2,1,0:T(8,128)(2,1)} %param.7) | copy-start | bytes 1572868
  1.7 1.0 %copy-start.2 = (bf16[1,128,2048]{2,1,0:T(8,128)(2,1)S(1)}, bf16[1,128,2048]{2,1,0:T(8,128)(2,1)}, u32[]{:S(2)}) copy-start(bf16[1,128,2048]{2,1,0:T(8,128)(2,1)} %param.10) | copy-start | bytes 1572868
  2.7 1.0 %copy-start.4 = (bf16[1,128,2048]{2,1,0:T(8,128)(2,1)S(1)}, bf16[1,128,2048]{2,1,0:T(8,128)(2,1)}, u32[]{:S(2)}) copy-start(bf16[1,128,2048]{2,1,0:T(8,128)(2,1)} %param.8) | copy-start | bytes 1572868
  3.8 1.0 %copy-start.6 = (bf16[1,128,2048]{2,1,0:T(8,128)(2,1)S(1)}, bf16[1,128,2048]{2,1,0:T(8,128)(2,1)}, u32[]{:S(2)}) copy-start(bf16[1,128,2048]{2,1,0:T(8,128)(2,1)} %param.9) | copy-start | bytes 1572868
  4.8 1.0 %copy-start.8 = (bf16[1,128,2048]{2,1,0:T(8,128)(2,1)S(1)}, bf16[1,128,2048]{2,1,0:T(8,128)(2,1)}, u32[]{:S(2)}) copy-start(bf16[1,128,2048]{2,1,0:T(8,128)(2,1)} %param.12) | copy-start | bytes 1572868
  5.8 1.0 %copy-start.10 = (f32[2048,64]{0,1:T(8,128)S(1)}, f32[2048,64]{0,1:T(8,128)}, u32[]{:S(2)}) copy-start(f32[2048,64]{0,1:T(8,128)} %param.13) | copy-start | bytes 1572868
  6.9 26.4 %copy-start.9 = (bf16[1,128,2048]{2,1,0:T(8,128)(2,1)S(1)}, bf16[1,128,2048]{2,1,0:T(8,128)(2,1)}, u32[]{:S(2)}) copy-start(bf16[1,128,2048]{2,1,0:T(8,128)(2,1)} %param.12) | copy-start | bytes 1572868
  9.7 9.7 %collective-permute-start.1 = (f32[17,32,128]{2,1,0:T(8,128)S(1)}, f32[17,32,128]{2,1,0:T(8,128)S(1)}, u32[]{:S(2)}, u32[]{:S(2)}) collective-permute-start(f32[17,32,128]{2,1,0:T(8,128)S(1)} %get-tuple-element.25), channel_id=1, source_target_pairs={{0,16},{16,0},{1,17},{17,1},{2,18},{18,2},{3,19},{19,3},{4,20},{20... | collective-permute-start | bytes 835592 | tf_op jit(solution)/shard_map/ppermute | solution.py:353
  19.4 13.9 %copy-start.7 = (bf16[1,128,2048]{2,1,0:T(8,128)(2,1)S(1)}, bf16[1,128,2048]{2,1,0:T(8,128)(2,1)}, u32[]{:S(2)}) copy-start(bf16[1,128,2048]{2,1,0:T(8,128)(2,1)} %param.9) | copy-start | bytes 1572868
  19.4 10.3 %copy-start.12 = (f32[32,64]{1,0:T(8,128)S(1)}, f32[32,64]{1,0:T(8,128)}, u32[]{:S(2)}) copy-start(f32[32,64]{1,0:T(8,128)} %param.11) | copy-start | bytes 24580
  19.4 13.8 %copy-start.5 = (bf16[1,128,2048]{2,1,0:T(8,128)(2,1)S(1)}, bf16[1,128,2048]{2,1,0:T(8,128)(2,1)}, u32[]{:S(2)}) copy-start(bf16[1,128,2048]{2,1,0:T(8,128)(2,1)} %param.8) | copy-start | bytes 1572868
  19.5 1.5 %collective-permute-start.2 = (f32[8,1,32,128]{3,2,0,1:T(8,128)S(1)}, f32[8,1,32,128]{3,2,0,1:T(8,128)}, u32[]{:S(2)}, u32[]{:S(2)}) collective-permute-start(f32[8,1,32,128]{3,2,0,1:T(8,128)S(1)} %select_bitcast_fusion), channel_id=1, source_target_pairs={{0,1},{1,0},{2,3},{3,2},{4,5},{5,4},{6,7},{7,6},{8,9},{9,8},{10,11... | collective-permute-start | bytes 393224 | tf_op jit(solution)/shard_map/ppermute | solution.py:368
  19.6 13.7 %copy-start.1 = (bf16[1,128,2048]{2,1,0:T(8,128)(2,1)S(1)}, bf16[1,128,2048]{2,1,0:T(8,128)(2,1)}, u32[]{:S(2)}) copy-start(bf16[1,128,2048]{2,1,0:T(8,128)(2,1)} %param.7) | copy-start | bytes 1572868
  19.6 13.7 %copy-start.3 = (bf16[1,128,2048]{2,1,0:T(8,128)(2,1)S(1)}, bf16[1,128,2048]{2,1,0:T(8,128)(2,1)}, u32[]{:S(2)}) copy-start(bf16[1,128,2048]{2,1,0:T(8,128)(2,1)} %param.10) | copy-start | bytes 1572868
  22.0 4.3 %collective-permute-start.3 = (f32[4,1,32,128]{3,2,0,1:T(8,128)S(1)}, f32[4,1,32,128]{3,2,0,1:T(8,128)S(1)}, u32[]{:S(2)}, u32[]{:S(2)}) collective-permute-start(f32[4,1,32,128]{3,2,0,1:T(8,128)S(1)} %select_bitcast_fusion.1), channel_id=1, source_target_pairs={{0,2},{1,3},{2,0},{3,1},{4,6},{5,7},{6,4},{7,5},{8,10},{9,11},{10,... | collective-permute-start | bytes 196616 | tf_op jit(solution)/shard_map/ppermute | solution.py:368
  26.4 4.0 %collective-permute-start.4 = (f32[2,1,32,128]{3,2,0,1:T(8,128)S(1)}, f32[2,1,32,128]{3,2,0,1:T(8,128)S(1)}, u32[]{:S(2)}, u32[]{:S(2)}) collective-permute-start(f32[2,1,32,128]{3,2,0,1:T(8,128)S(1)} %select_bitcast_fusion.2), channel_id=1, source_target_pairs={{0,4},{1,5},{2,6},{3,7},{4,0},{5,1},{6,2},{7,3},{8,12},{9,13},{10,... | collective-permute-start | bytes 98312 | tf_op jit(solution)/shard_map/ppermute | solution.py:368
  28.2 16.4 %collective-permute-start = (f32[16,64,128]{2,1,0:T(8,128)S(1)}, f32[16,64,128]{2,1,0:T(8,128)}, u32[]{:S(2)}, u32[]{:S(2)}) collective-permute-start(f32[16,64,128]{2,1,0:T(8,128)S(1)} %get-tuple-element.20), channel_id=1, source_target_pairs={{0,16},{16,0},{1,17},{17,1},{2,18},{18,2},{3,19},{19,3},{4,20},{20... | collective-permute-start | bytes 1572872 | tf_op jit(solution)/shard_map/ppermute | solution.py:354
  30.4 14.3 %copy-start.11 = (f32[2048,64]{0,1:T(8,128)S(1)}, f32[2048,64]{0,1:T(8,128)}, u32[]{:S(2)}) copy-start(f32[2048,64]{0,1:T(8,128)} %param.13) | copy-start | bytes 1572868
  30.4 13.7 %collective-permute-start.5 = (f32[1,1,32,128]{3,2,1,0:T(8,128)S(1)}, f32[1,1,32,128]{3,2,1,0:T(8,128)S(1)}, u32[]{:S(2)}, u32[]{:S(2)}) collective-permute-start(f32[1,1,32,128]{3,2,1,0:T(8,128)S(1)} %fusion.4), channel_id=1, source_target_pairs={{0,8},{1,9},{2,10},{3,11},{4,12},{5,13},{6,14},{7,15},{8,0},{9,1},... | collective-permute-start | bytes 49160 | tf_op jit(solution)/shard_map/ppermute | solution.py:368
where the time goes:
time: 49.7 us; the launch traced here: 49.2 us
  Pallas kernels  18.1 us (36%)
  starting transfers between devices  11.2 us (23%)
  waiting for transfers between devices  11.1 us (22%)
  local copies, waits for them, and re-layouts  6.36 us (13%)
  other arithmetic  1.67 us (3%)
  between operations  0.79 us (2%)
    pallas_call x1, Pallas kernels, inner(): pl.pallas_call(body, grid=grid, in_specs=[rows] * 5 + [pl.BlockSpec((1, b...  10.7 us
    ppermute x4, starting transfers between devices, on_device(): lax.ppermute(theirs, 'dp', [(i, i ^ bit) for i in range(dp_size)])  6.7 us
    ppermute x1, waiting for transfers between devices, on_device(): got = lax.ppermute(sent, 'seq', swap)  6.66 us
    unnamed x26, local copies, waits for them, and re-layouts  6.28 us
    pallas_call x1, Pallas kernels, outer(): pl.pallas_call(body, grid=grid, in_specs=[scalar] + [rows] * 8 + [wide, p...  4.56 us
    ppermute x4, waiting for transfers between devices, on_device(): lax.ppermute(theirs, 'dp', [(i, i ^ bit) for i in range(dp_size)])  4.45 us
    ppermute x1, starting transfers between devices, on_device(): got = lax.ppermute(sent, 'seq', swap)  3.03 us
    pallas_call x1, Pallas kernels, states(): pl.pallas_call(body, grid=grid, in_specs=[scalar] + [rows] * 5 + [wide],...  2.79 us
  transfers between devices with their start and end apart: 6, of which 4 were waited for; matrix products, arithmetic and copies ran while one was open for 1% of the time, Pallas kernels for 22%

commit v1 on v0

--- a/solution.py
+++ b/solution.py
@@ -5,8 +5,10 @@
 from jax.experimental.pallas import tpu as pltpu
 from jax.sharding import PartitionSpec as P
 
+
 LANES = 128
 CHUNK = 32
+UNROLL = 4
 BF16 = jnp.bfloat16
 F32 = jnp.float32
 
@@ -77,38 +79,64 @@
     return jnp.where(first_head((half, LANES)), x[:half], x[half:])
 
 
-def state_kernel(pairs, fast, flag, r, k, v, f, dy, init, *outs):
-    toks = r.shape[0]
+def state_kernel(group, fast, *refs):
+    sources, refs = refs[:6], refs[6:]
+    copies, refs = refs[:6], refs[6:]
+    outs, sems = refs[:-1], refs[-1]
+    r, k, v, f, dy, init = copies
+    toks, width = r.shape
+    steps = width // LANES // group
+    is_first = lax.axis_index("seq") == 0
+
+    def fetch(step, i):
+        lanes = pl.ds(step * group * LANES, group * LANES)
+        return pltpu.make_async_copy(
+            sources[i].at[:, lanes], copies[i].at[:, lanes], sems.at[step, i]
+        )
+
+    order = (3, 0, 4, 1, 2, 5)
+    for step in range(steps):
+        for i in order:
+            fetch(step, i).start()
     tri = triangles(toks)
-    step = pl.program_id(0)
-    for p in range(pairs):
-        at = slice(p * LANES, (p + 1) * LANES)
-        early, late, totals, _ = decays(f[:, at], tri)
-        from_start, to_end, whole = spread(early, late, totals)
-        key_hi, key_lo = split(k[:, at].astype(F32) * to_end)
-        rec_hi, rec_lo = split(r[:, at].astype(F32) * from_start)
-        state = dot(v[:, at], jnp.concatenate([key_hi, key_lo], 1), (0, 0))
-        grad = dot(dy[:, at], jnp.concatenate([rec_hi, rec_lo], 1), (0, 0))
-        state = diagonal(state[:, :LANES] + state[:, LANES:])
-        grad = diagonal(grad[:, :LANES] + grad[:, LANES:])
-        if fast:
-            sent, kept, swapped = outs
-            half = grad.shape[0] // 2
-            is_first = flag[0] == 0
-            end = whole * init[:, at] + state
-            swapped[p] = jnp.where(is_first, end, grad)
-            pair = step * pairs + p
-            sent[pair] = jnp.where(is_first, grad[half:], grad[:half])
-            kept[p] = jnp.where(is_first, grad[:half], grad[half:])
-            sent[sent.shape[0] - 1, pl.ds(pair, 1), :] = whole
-        else:
-            states, grads, wholes = outs
-            states[p] = state
-            grads[p] = grad
-            wholes[p] = whole
-
-
-def inner_kernel(pairs, r, k, v, f, dy, boost, rec, key, val, from_out, to_out):
+    for step in range(steps):
+        for i in order:
+            fetch(step, i).wait()
+        for pair in range(step * group, (step + 1) * group):
+            at = slice(pair * LANES, (pair + 1) * LANES)
+            early, late, totals, _ = decays(f[:, at], tri)
+            from_start, to_end, whole = spread(early, late, totals)
+            key_hi, key_lo = split(k[:, at].astype(F32) * to_end)
+            rec_hi, rec_lo = split(r[:, at].astype(F32) * from_start)
+            state = dot(v[:, at], jnp.concatenate([key_hi, key_lo], 1), (0, 0))
+            grad = dot(dy[:, at], jnp.concatenate([rec_hi, rec_lo], 1), (0, 0))
+            state = diagonal(state[:, :LANES] + state[:, LANES:])
+            grad = diagonal(grad[:, :LANES] + grad[:, LANES:])
+            if fast:
+                sent, kept, swapped = outs
+                half = grad.shape[0] // 2
+                end = whole * init[:, at] + state
+                swapped[pair] = jnp.where(is_first, end, grad)
+                sent[pair] = jnp.where(is_first, grad[half:], grad[:half])
+                kept[pair] = jnp.where(is_first, grad[:half], grad[half:])
+                sent[sent.shape[0] - 1, pair : pair + 1] = whole
+            else:
+                states, grads, wholes = outs
+                states[pair] = state
+                grads[pair] = grad
+                wholes[pair] = whole
+
+
+def inner_kernel(first, count, unroll, r, k, v, f, dy, boost, *outs):
+    def step(i, carry):
+        base = pl.multiple_of(i * unroll * LANES, LANES)
+        inner_pairs(first * LANES + base, base, unroll, r, k, v, f, dy, boost, *outs)
+        return carry
+
+    lax.fori_loop(0, count // unroll, step, 0)
+
+
+def inner_pairs(base, out_base, pairs, r, k, v, f, dy, boost, rec, key, val, from_out, to_out):
     toks = r.shape[0]
     chunks = toks // CHUNK
     tri = triangles(toks)
@@ -129,14 +157,16 @@
 
     rows = [slice(c * CHUNK, (c + 1) * CHUNK) for c in range(chunks)]
     for p in range(pairs):
-        at = slice(p * LANES, (p + 1) * LANES)
+        at = pl.ds(pl.multiple_of(base + p * LANES, LANES), LANES)
+        to = pl.ds(pl.multiple_of(out_base + p * LANES, LANES), LANES)
         early, late, totals, middles = decays(f[:, at], tri)
         from_start, to_end, _ = spread(early, late, totals)
-        from_out[:, at] = from_start
-        to_out[:, at] = to_end
+        from_out[:, to] = from_start
+        to_out[:, to] = to_end
         rb, kb, vb, db = r[:, at], k[:, at], v[:, at], dy[:, at]
         rf, kf, vf, df = (x.astype(F32) for x in (rb, kb, vb, db))
-        u = boost[:, at]
+        head = 2 * (base // LANES + p)
+        u = jnp.concatenate([boost[pl.ds(head, 1)], boost[pl.ds(head + 1, 1)]], 1)
         rec_early = rf * early
         key_late = kf * late
         dy_heads = by_head(flip(db))
@@ -207,73 +237,93 @@
             return jnp.where(keep, one, two)
 
         boosted = u * head_sum(prod)
-        rec[:, at] = jnp.concatenate(rec_rows, 0) + kf * boosted
-        key[:, at] = jnp.concatenate(key_rows, 0) + rf * boosted
-        val[:, at] = inner_val + head_sum(mix) * df
+        rec[:, to] = jnp.concatenate(rec_rows, 0) + kf * boosted
+        key[:, to] = jnp.concatenate(key_rows, 0) + rf * boosted
+        val[:, to] = inner_val + head_sum(mix) * df
 
 
 def outer_kernel(
-    pairs, fast, flag, k, v, dy, from_start, to_end, rec, key, val, init, state, grad, *outs
+    first, pairs, fast, k, v, dy, from_start, to_end, rec, key, val, init, *refs
 ):
-    rec_out, key_out, val_out = outs
+    state, grad = refs[0], refs[-4]
+    rec_out, key_out, val_out = refs[-3:]
+    is_first = lax.axis_index("seq") == 0
+    step = pl.program_id(0)
     for p in range(pairs):
-        at = slice(p * LANES, (p + 1) * LANES)
+        here = step * pairs + p
+        at = pl.ds(pl.multiple_of((first + here) * LANES, LANES), LANES)
+        part = pl.ds(pl.multiple_of(here * LANES, LANES), LANES)
+        out = slice(p * LANES, (p + 1) * LANES)
         if fast:
-            is_first = flag[0] == 0
-            got = state[p]
+            got = state[first + here]
             start = jnp.where(is_first, init[:, at], got)
             after = jnp.where(is_first, got, 0.0)
         else:
-            start = state[p]
-            after = grad[p]
+            start = state[first + here]
+            after = grad[first + here]
         start_hi, start_lo = split(by_head(start))
         after_hi, after_lo = split(by_head(after))
         db, vb = dy[:, at], v[:, at]
         from_state = dot(
             jnp.concatenate([db, db], 1), jnp.concatenate([start_hi, start_lo], 0)
         )
-        rec_out[:, at] = (rec[:, at] + from_start[:, at] * from_state).astype(BF16)
+        rec_out[:, out] = (rec[:, part] + from_start[:, part] * from_state).astype(BF16)
         from_grad = dot(jnp.concatenate([vb, vb], 1), jnp.concatenate([after_hi, after_lo], 0))
-        tail = to_end[:, at]
-        key_out[:, at] = (key[:, at] + tail * from_grad).astype(BF16)
+        tail = to_end[:, part]
+        key_out[:, out] = (key[:, part] + tail * from_grad).astype(BF16)
         key_hi, key_lo = split(k[:, at].astype(F32) * tail)
         wide = dot(key_hi, jnp.concatenate([after_hi, after_lo], 0), (1, 1))
         from_key = wide[:, :LANES] + wide[:, LANES:] + dot(key_lo, after_hi, (1, 1))
-        val_out[:, at] = (val[:, at] + from_key).astype(BF16)
+        val_out[:, out] = (val[:, part] + from_key).astype(BF16)
+
+
+def share_kernel(blocks, sent, kept, got, mine, theirs):
+    is_first = lax.axis_index("seq") == 0
+    upper = lax.axis_index("dp") & 1
+    last = sent.shape[0] - 1
+    for b in range(blocks // 2):
+        for ref, low in ((mine, upper), (theirs, 1 - upper)):
+            p = 2 * b + low
+            whole = jnp.where(is_first, sent[last, pl.ds(p, 1), :], got[last, pl.ds(p, 1), :])
+            own, other = kept[p], got[p]
+            ref[b] = jnp.where(is_first, own, other) + whole * jnp.where(is_first, other, own)
+
+
+def halve_kernel(bit, mine, got, kept, theirs):
+    upper = (lax.axis_index("dp") // bit) & 1
+    for b in range(kept.shape[0]):
+        for ref, low in ((kept, upper), (theirs, 1 - upper)):
+            ref[b] = mine[2 * b + low] + got[2 * b + low]
 
 
 def on_device(seq_size, dp_size, r, k, v, f, boost, dy, init):
     batch, toks, width = r.shape
-    heads, feature = boost.shape
+    _, feature = boost.shape
     pairs = width // LANES
     group = 4 if pairs % 4 == 0 else 1
-    grid = (pairs // group,)
     half = feature // 2
-    block = group * LANES
     fast = (
         batch == 1
         and seq_size == 2
         and dp_size & (dp_size - 1) == 0
-        and pairs % dp_size == 0
+        and pairs == dp_size
         and pairs <= half
     )
     seq = lax.axis_index("seq")
     is_first = seq == 0
-    flag = jnp.reshape(seq, (1,)).astype(jnp.int32)
-    boost_row = boost.reshape(1, width)
     init_t = init.T
 
-    rows = pl.BlockSpec((toks, block), lambda i: (0, i))
-    wide = pl.BlockSpec((feature, block), lambda i: (0, i))
-    per_pair = pl.BlockSpec((group, feature, LANES), lambda i: (i, 0, 0))
-    half_pair = pl.BlockSpec((group, half, LANES), lambda i: (i, 0, 0))
-    scalar = pl.BlockSpec(memory_space=pltpu.SMEM)
-    params = pltpu.CompilerParams(
-        dimension_semantics=("arbitrary",), vmem_limit_bytes=24 * 2**20
-    )
+    vmem = pl.BlockSpec(memory_space=pltpu.VMEM)
+    anywhere = pl.BlockSpec(memory_space=pl.ANY)
+
+    def limit(mib):
+        return pltpu.CompilerParams(vmem_limit_bytes=mib * 2**20)
 
     def like(shape, kind=F32):
         return jax.ShapeDtypeStruct(shape, kind)
+
+    def in_hbm(x):
+        return pltpu.with_memory_space_constraint(x, pltpu.HBM)
 
     def states(b):
         if fast:
@@ -282,95 +332,110 @@
                 like((pairs, half, LANES)),
                 like((pairs, feature, LANES)),
             )
-            specs = (
-                pl.BlockSpec((pairs + 1, half, LANES), lambda i: (0, 0, 0)),
-                half_pair,
-                per_pair,
-            )
         else:
             shapes = (
                 like((pairs, feature, LANES)),
                 like((pairs, feature, LANES)),
                 like((pairs, 1, LANES)),
             )
-            specs = (per_pair, per_pair, pl.BlockSpec((group, 1, LANES), lambda i: (i, 0, 0)))
-
-        def body(*refs):
-            state_kernel(group, fast, *refs)
-
-        return pl.pallas_call(
-            body,
-            grid=grid,
-            in_specs=[scalar] + [rows] * 5 + [wide],
-            out_specs=specs,
-            out_shape=shapes,
-            compiler_params=params,
+        operands = (r[b], k[b], v[b], f[b], dy[b], init_t)
+        outs = pl.pallas_call(
+            lambda *refs: state_kernel(group, fast, *refs),
+            in_specs=[anywhere] * 6,
+            out_specs=(vmem,) * 9,
+            out_shape=tuple(like(x.shape, x.dtype) for x in operands) + shapes,
+            scratch_shapes=[pltpu.SemaphoreType.DMA((pairs // group, 6))],
+            compiler_params=limit(24),
             name="states",
             cost_estimate=pl.CostEstimate(
                 flops=4 * 10**9, bytes_accessed=4 * 2**20, transcendentals=10**6
             ),
-        )(flag, r[b], k[b], v[b], f[b], dy[b], init_t)
-
-    def inner(b):
+        )(*(in_hbm(x) for x in operands))
+        return outs[:6], outs[6:]
+
+    def inner(near, first=0, count=pairs):
         def body(*refs):
-            inner_kernel(group, *refs)
+            inner_kernel(first, count, UNROLL if count % UNROLL == 0 else 1, *refs)
 
         return pl.pallas_call(
             body,
-            grid=grid,
-            in_specs=[rows] * 5 + [pl.BlockSpec((1, block), lambda i: (0, i))],
-            out_specs=(rows,) * 5,
-            out_shape=(like((toks, width)),) * 5,
-            compiler_params=params,
+            in_specs=[vmem] * 6,
+            out_specs=(vmem,) * 5,
+            out_shape=(like((toks, count * LANES)),) * 5,
+            compiler_params=limit(24),
             name="inner",
             cost_estimate=pl.CostEstimate(
                 flops=10**10, bytes_accessed=8 * 2**20, transcendentals=10**6
             ),
-        )(r[b], k[b], v[b], f[b], dy[b], boost_row)
-
-    def outer(b, partial, state, grad):
+        )(*near[:5], boost)
+
+    def outer(near, partial, carried, first=0, count=pairs, prior=()):
         rec, key, val, from_start, to_end = partial
+        _, k, v, _, dy, start = near
+        group = 4 if count % 4 == 0 else 1
+        block = group * LANES
 
         def body(*refs):
-            outer_kernel(group, fast, *refs)
-
+            given = 9 + len(carried)
+            outer_kernel(first, group, fast, *refs[:given], *refs[given + len(prior) :])
+
+        here = pl.BlockSpec((toks, block), lambda i: (0, i + first // group))
         return pl.pallas_call(
             body,
-            grid=grid,
-            in_specs=[scalar] + [rows] * 8 + [wide, per_pair, per_pair],
-            out_specs=(rows,) * 3,
+            grid=(count // group,),
+            in_specs=[vmem] * (9 + len(carried)) + [anywhere] * len(prior),
+            out_specs=(here,) * 3,
             out_shape=(like((toks, width), BF16),) * 3,
-            compiler_params=params,
+            input_output_aliases={9 + len(carried) + i: i for i in range(len(prior))},
+            compiler_params=limit(24),
             name="outer",
             cost_estimate=pl.CostEstimate(
                 flops=3 * 10**9, bytes_accessed=9 * 2**20, transcendentals=0
             ),
-        )(flag, k[b], v[b], dy[b], from_start, to_end, rec, key, val, init_t, state, grad)
+        )(k, v, dy, from_start, to_end, rec, key, val, start, *carried, *prior)
+
+    def share(sent, kept, got):
+        shape = like((pairs // 2, half, LANES))
+        return pl.pallas_call(
+            lambda *refs: share_kernel(pairs, *refs),
+            in_specs=[vmem] * 3,
+            out_specs=(vmem,) * 2,
+            out_shape=(shape,) * 2,
+            compiler_params=limit(2),
+            name="share",
+        )(sent, kept, got)
+
+    def halve(bit, mine, got):
+        shape = like((mine.shape[0] // 2,) + mine.shape[1:])
+        return pl.pallas_call(
+            lambda *refs: halve_kernel(bit, *refs),
+            in_specs=[vmem] * 2,
+            out_specs=(vmem,) * 2,
+            out_shape=(shape,) * 2,
+            compiler_params=limit(2),
+            name="halve",
+        )(mine, got)
 
     if fast:
-        sent, kept, swapped = states(0)
+        near, (sent, kept, swapped) = states(0)
         swap = [(0, 1), (1, 0)]
         got = lax.ppermute(sent, "seq", swap)
         other = lax.ppermute(swapped, "seq", swap)
-        partial = inner(0)
-        whole = jnp.where(is_first, sent[pairs, :pairs], got[pairs, :pairs])[:, None, :]
-        total = jnp.where(is_first, kept, got[:pairs]) + whole * jnp.where(
-            is_first, got[:pairs], kept
-        )
-        place = lax.axis_index("dp")
-        total = total.reshape(dp_size, pairs // dp_size, half, LANES)
+        cut = 3 * pairs // 4
+        partial_a = inner(near, 0, cut)
+        partial_b = inner(near, cut, pairs - cut)
+        mine, theirs = share(sent, kept, got)
         bit = 1
-        while bit < dp_size:
-            couples = total.reshape((total.shape[0] // 2, 2) + total.shape[1:])
-            upper = (place & bit) != 0
-            mine = jnp.where(upper, couples[:, 1], couples[:, 0])
-            theirs = jnp.where(upper, couples[:, 0], couples[:, 1])
-            total = mine + lax.ppermute(
-                theirs, "dp", [(i, i ^ bit) for i in range(dp_size)]
-            )
+        while True:
+            got = lax.ppermute(theirs, "dp", [(i, i ^ bit) for i in range(dp_size)])
             bit *= 2
-        state_grad = total[0].transpose(0, 2, 1).reshape(-1, half)
-        rec, key, val = outer(0, partial, other, other)
+            if bit == dp_size:
+                break
+            mine, theirs = halve(bit, mine, got)
+        total = mine + got
+        state_grad = total.transpose(0, 2, 1).reshape(-1, half)
+        results = outer(near, partial_a, (other,), 0, cut)
+        rec, key, val = outer(near, partial_b, (other,), cut, pairs - cut, results)
         return rec[None], key[None], val[None], state_grad
 
     forward = [(i, i + 1) for i in range(seq_size - 1)]
@@ -378,14 +443,14 @@
     start_t = init_t.reshape(feature, pairs, LANES).transpose(1, 0, 2)
     results, term = [], 0.0
     for b in range(batch):
-        state_local, grad_local, whole = states(b)
+        near, (state_local, grad_local, whole) = states(b)
         start = start_t
         after = jnp.zeros_like(grad_local)
         for _ in range(seq_size - 1):
             end = whole * start + state_local
             start = jnp.where(is_first, start_t, lax.ppermute(end, "seq", forward))
             after = lax.ppermute(grad_local + whole * after, "seq", backward)
-        results.append(outer(b, inner(b), start, after))
+        results.append(outer(near, inner(near), (start, after)))
         term = term + jnp.where(is_first, grad_local + whole * after, 0.0)
     term = term.transpose(0, 2, 1).reshape(width, feature)
     summed = lax.psum_scatter(term, "dp", scatter_dimension=0, tiled=True)

time: 49.7 us -> 39.1 us (0.79)
  local copies, waits for them, and re-layouts: 6.36 us -> 0.01 us
  waiting for transfers between devices: 11.1 us -> 9 us
  other arithmetic: 1.67 us -> 0.61 us
  Pallas kernels: 18.1 us -> 17.6 us
    unnamed x26 -> x2, local copies, waits for them, and re-layouts: 6.28 us -> 0.01 us
    ppermute x4, waiting for transfers between devices: 4.45 us -> 2.34 us  [on_device(): got = lax.ppermute(theirs, 'dp', [(i, i ^ bit) for i in range(dp_size)])]
    add x4 -> x0, other arithmetic: 1.01 us -> none  [the longest x3 0.96 us: on_device(): mine + lax.ppermute(theirs, 'dp', [(i, i ^ bit) for i in range(dp_size)])]
    pallas_call x3 -> x9, Pallas kernels: 18.1 us -> 17.6 us  [the longest x2 10.1 us: inner(): pl.pallas_call(body, in_specs=[vmem] * 6, out_specs=(vmem,) * 5, out_shap...]
  transfers between devices with their start and end apart: 6 -> 6, of which waited for: 4 -> 3; matrix products, arithmetic and copies ran while one was open for 1% -> 2% of each run, Pallas kernels for 22% -> 26%
where the time goes in v1:
time: 39.1 us; the launch traced here: 38.9 us
  Pallas kernels  17.6 us (45%)
  starting transfers between devices  11 us (28%)
  waiting for transfers between devices  9 us (23%)
  between operations  0.71 us (2%)
  other arithmetic  0.61 us (2%)
    pallas_call x2, Pallas kernels, inner(): pl.pallas_call(body, in_specs=[vmem] * 6, out_specs=(vmem,) * 5, out_shap...  10.1 us
    ppermute x1, waiting for transfers between devices, on_device(): got = lax.ppermute(sent, 'seq', swap)  6.66 us
    ppermute x4, starting transfers between devices, on_device(): got = lax.ppermute(theirs, 'dp', [(i, i ^ bit) for i in range(dp_size)])  6.45 us
    pallas_call x1, Pallas kernels, states(): pl.pallas_call(lambda *refs: state_kernel(group, fast, *refs), in_specs=[...  3.93 us
    pallas_call x2, Pallas kernels, outer(): pl.pallas_call(body, grid=(count // group,), in_specs=[vmem] * (9 + len(c...  3.49 us
    ppermute x1, starting transfers between devices, on_device(): got = lax.ppermute(sent, 'seq', swap)  3.03 us
    ppermute x4, waiting for transfers between devices, on_device(): got = lax.ppermute(theirs, 'dp', [(i, i ^ bit) for i in range(dp_size)])  2.34 us
    ppermute x1, starting transfers between devices, on_device(): other = lax.ppermute(swapped, 'seq', swap)  1.49 us
  transfers between devices with their start and end apart: 6, of which 3 were waited for; matrix products, arithmetic and copies ran while one was open for 2% of the time, Pallas kernels for 26%

profile of v1, /device:TPU:0, one launch (start us, length us, event | category | flops | bytes accessed | tf_op | source)
XLA Modules:
  0.0 38.9 jit_solution(1867860292686602092)
XLA Ops:
  0.6 3.9 %states.1 = (bf16[128,2048]{1,0:T(8,128)(2,1)S(1)}, bf16[128,2048]{1,0:T(8,128)(2,1)S(1)}, bf16[128,2048]{1,0:T(8,128)(2,1)S(1)}, bf16[128,2048]{1,0:T(8,128)(2,...) custom-call(bf16[128,2048]{1,0:T(8,128)(2,1)} %bitcast.13, ...), custom_call_target="tpu_custom_call" | custom-call | flops 4000000000 | bytes 4194304 | tf_op jit(solution)/shard_map/states/pallas_call | solution.py:342
  4.6 3.0 %collective-permute-start.1 = (f32[17,32,128]{2,1,0:T(8,128)S(1)}, f32[17,32,128]{2,1,0:T(8,128)S(1)}, u32[]{:S(2)}, u32[]{:S(2)}) collective-permute-start(f32[17,32,128]{2,1,0:T(8,128)S(1)} %get-tuple-element.60.refs_0_), channel_id=1, source_target_pairs={{0,16},{16,0},{1,17},{17,1},{2,18},{18,2},{3,19},{19,3},{4,20},{20... | collective-permute-start | bytes 835592 | tf_op jit(solution)/shard_map/ppermute | solution.py:422
  7.6 6.7 %collective-permute-done.1.refs_2_ = f32[17,32,128]{2,1,0:T(8,128)S(1)} collective-permute-done((f32[17,32,128]{2,1,0:T(8,128)S(1)}, f32[17,32,128]{2,1,0:T(8,128)S(1)}, u32[]{:S(2)}, u32[]{:S(2)}) %collective-permute-start.1) | collective-permute-done | bytes 278560 | tf_op jit(solution)/shard_map/ppermute | solution.py:422
  14.3 0.1 collective-permute-start.2
  14.4 1.3 %collective-permute-done.2.refs_1_ = f32[8,32,128]{2,1,0:T(8,128)S(1)} collective-permute-done((f32[8,32,128]{2,1,0:T(8,128)S(1)}, f32[8,32,128]{2,1,0:T(8,128)S(1)}, u32[]{:S(2)}, u32[]{:S(2)}) %collective-permute-start.2) | collective-permute-done | bytes 131104 | tf_op jit(solution)/shard_map/ppermute | solution.py:430
  15.7 1.8 %collective-permute-start.3 = (f32[4,32,128]{2,1,0:T(8,128)S(1)}, f32[4,32,128]{2,1,0:T(8,128)S(1)}, u32[]{:S(2)}, u32[]{:S(2)}) collective-permute-start(f32[4,32,128]{2,1,0:T(8,128)S(1)} %get-tuple-element.65), channel_id=1, source_target_pairs={{0,2},{1,3},{2,0},{3,1},{4,6},{5,7},{6,4},{7,5},{8,10},{9,11},{10,... | collective-permute-start | bytes 196616 | tf_op jit(solution)/shard_map/ppermute | solution.py:430
  17.6 1.5 %collective-permute-start = (f32[16,64,128]{2,1,0:T(8,128)S(1)}, f32[16,64,128]{2,1,0:T(8,128)S(1)}, u32[]{:S(2)}, u32[]{:S(2)}) collective-permute-start(f32[16,64,128]{2,1,0:T(8,128)S(1)} %get-tuple-element.48), channel_id=1, source_target_pairs={{0,16},{16,0},{1,17},{17,1},{2,18},{18,2},{3,19},{19,3},{4,20},{20... | collective-permute-start | bytes 1572872 | tf_op jit(solution)/shard_map/ppermute | solution.py:423
  19.1 1.0 %collective-permute-done.3.refs_1_ = f32[4,32,128]{2,1,0:T(8,128)S(1)} collective-permute-done((f32[4,32,128]{2,1,0:T(8,128)S(1)}, f32[4,32,128]{2,1,0:T(8,128)S(1)}, u32[]{:S(2)}, u32[]{:S(2)}) %collective-permute-start.3) | collective-permute-done | bytes 65568 | tf_op jit(solution)/shard_map/ppermute | solution.py:430
  20.1 0.0 copy-start
  20.1 1.9 %collective-permute-start.4 = (f32[2,32,128]{2,1,0:T(8,128)S(1)}, f32[2,32,128]{2,1,0:T(8,128)S(1)}, u32[]{:S(2)}, u32[]{:S(2)}) collective-permute-start(f32[2,32,128]{2,1,0:T(8,128)S(1)} %get-tuple-element.67), channel_id=1, source_target_pairs={{0,4},{1,5},{2,6},{3,7},{4,0},{5,1},{6,2},{7,3},{8,12},{9,13},{10,... | collective-permute-start | bytes 98312 | tf_op jit(solution)/shard_map/ppermute | solution.py:430
  22.0 0.0 copy-done
  22.0 7.6 %inner.3 = (f32[128,1536]{1,0:T(8,128)S(1)}, f32[128,1536]{1,0:T(8,128)S(1)}, f32[128,1536]{1,0:T(8,128)S(1)}, f32[128,1536]{1,0:T(8,128)S(1)}, f32[128,1536]{1,0:T(8,128)S(1)}) custom-call(bf16[128,2048]{1,0:T(8,128)(2,1)S(1)} %get-tuple-element.40.refs_0_, bf16[128,2048]{1,0:T(8,128)(2,1)S(1)} %get-tuple-element.37.refs_1_.refs_0_, ...), custom_call_target="tpu_custom_call" | custom-call | flops 10000000000 | bytes 8388608 | tf_op jit(solution)/shard_map/inner/pallas_call | solution.py:360
  29.6 0.0 collective-permute-done.4.refs_1_
  29.6 2.7 %collective-permute-start.5 = (f32[1,32,128]{2,1,0:T(8,128)S(1)}, f32[1,32,128]{2,1,0:T(8,128)S(1)}, u32[]{:S(2)}, u32[]{:S(2)}) collective-permute-start(f32[1,32,128]{2,1,0:T(8,128)S(1)} %get-tuple-element.69), channel_id=1, source_target_pairs={{0,8},{1,9},{2,10},{3,11},{4,12},{5,13},{6,14},{7,15},{8,0},{9,1},... | collective-permute-start | bytes 49160 | tf_op jit(solution)/shard_map/ppermute | solution.py:430
  32.3 2.5 %inner.2 = (f32[128,512]{1,0:T(8,128)S(1)}, f32[128,512]{1,0:T(8,128)S(1)}, f32[128,512]{1,0:T(8,128)S(1)}, f32[128,512]{1,0:T(8,128)S(1)}, f32[128,512]{1,0:T(8,128)S(1)}) custom-call(bf16[128,2048]{1,0:T(8,128)(2,1)S(1)} %get-tuple-element.40.refs_0_, bf16[128,2048]{1,0:T(8,128)(2,1)S(1)} %get-tuple-element.37.refs_1_.refs_0_, ...), custom_call_target="tpu_custom_call" | custom-call | flops 10000000000 | bytes 8388608 | tf_op jit(solution)/shard_map/inner/pallas_call | solution.py:360
  34.8 0.0 collective-permute-done.5
  34.8 0.6 %add_bitcast_fusion = f32[128,32]{0,1:T(8,128)} fusion(f32[1,32,128]{2,1,0:T(8,128)S(1)} %get-tuple-element.68, f32[1,32,128]{2,1,0:T(8,128)S(1)} %collective-permute-done.5), kind=kLoop, calls=%fused_computation | loop fusion | flops 4096 | bytes 49152 | tf_op jit(solution)/shard_map/reshape | solution.py:436
  35.4 0.0 collective-permute-done.refs_9_
  35.4 2.4 %outer.2 = (bf16[128,2048]{1,0:T(8,128)(2,1)}, bf16[128,2048]{1,0:T(8,128)(2,1)}, bf16[128,2048]{1,0:T(8,128)(2,1)}) custom-call(bf16[128,2048]{1,0:T(8,128)(2,1)S(1)} %get-tuple-element.37.refs_1_.refs_0_, bf16[128,2048]{1,0:T(8,128)(2,1)S(1)} %get-tuple-element.38.refs_2_.refs_1_, bf16[128,2048]{1,0:T(8,128)(2,1)S(1)} %get-tuple-element.39.refs_4_.refs_2_, ...), custom_call_target="tpu_custom_call" | custom-call | flops 3000000000 | bytes 9437184 | tf_op jit(solution)/shard_map/outer/pallas_call | solution.py:383
  37.8 1.1 %outer.3 = (bf16[128,2048]{1,0:T(8,128)(2,1)}, bf16[128,2048]{1,0:T(8,128)(2,1)}, bf16[128,2048]{1,0:T(8,128)(2,1)}) custom-call(bf16[128,2048]{1,0:T(8,128)(2,1)S(1)} %get-tuple-element.37.refs_1_.refs_0_, bf16[128,2048]{1,0:T(8,128)(2,1)S(1)} %get-tuple-element.38.refs_2_.refs_1_, ...), custom_call_target="tpu_custom_call", output_to_operand_aliasing={{0}: (10, {}), {1}: (11, {}), {2}: (12, {})} | custom-call | flops 3000000000 | bytes 9437184 | tf_op jit(solution)/shard_map/outer/pallas_call | solution.py:383
  (4 shorter events, 0.1 us)
Async XLA Ops:
  4.6 9.7 %collective-permute-start.1 = (f32[17,32,128]{2,1,0:T(8,128)S(1)}, f32[17,32,128]{2,1,0:T(8,128)S(1)}, u32[]{:S(2)}, u32[]{:S(2)}) collective-permute-start(f32[17,32,128]{2,1,0:T(8,128)S(1)} %get-tuple-element.60.refs_0_), channel_id=1, source_target_pairs={{0,16},{16,0},{1,17},{17,1},{2,18},{18,2},{3,19},{19,3},{4,20},{20... | collective-permute-start | bytes 835592 | tf_op jit(solution)/shard_map/ppermute | solution.py:422
  14.3 1.4 %collective-permute-start.2 = (f32[8,32,128]{2,1,0:T(8,128)S(1)}, f32[8,32,128]{2,1,0:T(8,128)S(1)}, u32[]{:S(2)}, u32[]{:S(2)}) collective-permute-start(f32[8,32,128]{2,1,0:T(8,128)S(1)} %get-tuple-element.63), channel_id=1, source_target_pairs={{0,1},{1,0},{2,3},{3,2},{4,5},{5,4},{6,7},{7,6},{8,9},{9,8},{10,11... | collective-permute-start | bytes 393224 | tf_op jit(solution)/shard_map/ppermute | solution.py:430
  15.7 4.3 %collective-permute-start.3 = (f32[4,32,128]{2,1,0:T(8,128)S(1)}, f32[4,32,128]{2,1,0:T(8,128)S(1)}, u32[]{:S(2)}, u32[]{:S(2)}) collective-permute-start(f32[4,32,128]{2,1,0:T(8,128)S(1)} %get-tuple-element.65), channel_id=1, source_target_pairs={{0,2},{1,3},{2,0},{3,1},{4,6},{5,7},{6,4},{7,5},{8,10},{9,11},{10,... | collective-permute-start | bytes 196616 | tf_op jit(solution)/shard_map/ppermute | solution.py:430
  17.6 17.9 %collective-permute-start = (f32[16,64,128]{2,1,0:T(8,128)S(1)}, f32[16,64,128]{2,1,0:T(8,128)S(1)}, u32[]{:S(2)}, u32[]{:S(2)}) collective-permute-start(f32[16,64,128]{2,1,0:T(8,128)S(1)} %get-tuple-element.48), channel_id=1, source_target_pairs={{0,16},{16,0},{1,17},{17,1},{2,18},{18,2},{3,19},{19,3},{4,20},{20... | collective-permute-start | bytes 1572872 | tf_op jit(solution)/shard_map/ppermute | solution.py:423
  20.1 1.9 %copy-start = (f32[32,64]{1,0:T(8,128)S(1)}, f32[32,64]{1,0:T(8,128)}, u32[]{:S(2)}) copy-start(f32[32,64]{1,0:T(8,128)} %refs_5_.3) | copy-start | bytes 24580
  20.1 9.5 %collective-permute-start.4 = (f32[2,32,128]{2,1,0:T(8,128)S(1)}, f32[2,32,128]{2,1,0:T(8,128)S(1)}, u32[]{:S(2)}, u32[]{:S(2)}) collective-permute-start(f32[2,32,128]{2,1,0:T(8,128)S(1)} %get-tuple-element.67), channel_id=1, source_target_pairs={{0,4},{1,5},{2,6},{3,7},{4,0},{5,1},{6,2},{7,3},{8,12},{9,13},{10,... | collective-permute-start | bytes 98312 | tf_op jit(solution)/shard_map/ppermute | solution.py:430
  29.6 5.2 %collective-permute-start.5 = (f32[1,32,128]{2,1,0:T(8,128)S(1)}, f32[1,32,128]{2,1,0:T(8,128)S(1)}, u32[]{:S(2)}, u32[]{:S(2)}) collective-permute-start(f32[1,32,128]{2,1,0:T(8,128)S(1)} %get-tuple-element.69), channel_id=1, source_target_pairs={{0,8},{1,9},{2,10},{3,11},{4,12},{5,13},{6,14},{7,15},{8,0},{9,1},... | collective-permute-start | bytes 49160 | tf_op jit(solution)/shard_map/ppermute | solution.py:430

commit v2 on v1

--- a/solution.py
+++ b/solution.py
@@ -242,39 +242,112 @@
         val[:, to] = inner_val + head_sum(mix) * df
 
 
-def outer_kernel(
-    first, pairs, fast, k, v, dy, from_start, to_end, rec, key, val, init, *refs
-):
-    state, grad = refs[0], refs[-4]
-    rec_out, key_out, val_out = refs[-3:]
+def state_part(rows, state):
+    hi, lo = split(by_head(state))
+    return dot(jnp.concatenate([rows, rows], 1), jnp.concatenate([hi, lo], 0))
+
+
+def key_part(keys, state):
+    hi, lo = split(by_head(state))
+    key_hi, key_lo = split(keys)
+    wide = dot(key_hi, jnp.concatenate([hi, lo], 0), (1, 1))
+    return wide[:, :LANES] + wide[:, LANES:] + dot(key_lo, hi, (1, 1))
+
+
+def outer_kernel(pairs, k, v, dy, from_start, to_end, rec, key, val, start, after, *outs):
+    rec_out, key_out, val_out = outs
+    for p in range(pairs):
+        at = slice(p * LANES, (p + 1) * LANES)
+        tail = to_end[:, at]
+        from_state = state_part(dy[:, at], start[p])
+        rec_out[:, at] = (rec[:, at] + from_start[:, at] * from_state).astype(BF16)
+        from_grad = state_part(v[:, at], after[p])
+        key_out[:, at] = (key[:, at] + tail * from_grad).astype(BF16)
+        from_key = key_part(k[:, at].astype(F32) * tail, after[p])
+        val_out[:, at] = (val[:, at] + from_key).astype(BF16)
+
+
+class Writer:
+    def __init__(self, group, held, outs, sems):
+        self.group, self.held, self.outs, self.sems = group, held, outs, sems
+        self.started = []
+
+    def put(self, pair, *values):
+        at = slice(pair * LANES, (pair + 1) * LANES)
+        for i, value in enumerate(values):
+            self.held[i, :, at] = value.astype(BF16)
+        if (pair + 1) % self.group == 0:
+            step = pair // self.group
+            lanes = pl.ds(step * self.group * LANES, self.group * LANES)
+            for i in range(len(values)):
+                copy = pltpu.make_async_copy(
+                    self.held.at[i, :, lanes], self.outs[i].at[:, lanes], self.sems.at[step, i]
+                )
+                copy.start()
+                self.started.append(copy)
+
+    def finish(self):
+        for copy in self.started:
+            copy.wait()
+
+
+def partial_of(pair, early, late):
+    count = early[0].shape[1] // LANES
+    refs, place = (early, pair) if pair < count else (late, pair - count)
+    return refs, slice(place * LANES, (place + 1) * LANES)
+
+
+def known_kernel(group, dy, init, *refs):
+    early, late, (rec_out, key_out, val_out, held, sems) = refs[:5], refs[5:10], refs[10:]
+    pairs = dy.shape[1] // LANES
     is_first = lax.axis_index("seq") == 0
-    step = pl.program_id(0)
-    for p in range(pairs):
-        here = step * pairs + p
-        at = pl.ds(pl.multiple_of((first + here) * LANES, LANES), LANES)
-        part = pl.ds(pl.multiple_of(here * LANES, LANES), LANES)
-        out = slice(p * LANES, (p + 1) * LANES)
-        if fast:
-            got = state[first + here]
-            start = jnp.where(is_first, init[:, at], got)
-            after = jnp.where(is_first, got, 0.0)
-        else:
-            start = state[first + here]
-            after = grad[first + here]
-        start_hi, start_lo = split(by_head(start))
-        after_hi, after_lo = split(by_head(after))
-        db, vb = dy[:, at], v[:, at]
-        from_state = dot(
-            jnp.concatenate([db, db], 1), jnp.concatenate([start_hi, start_lo], 0)
-        )
-        rec_out[:, out] = (rec[:, part] + from_start[:, part] * from_state).astype(BF16)
-        from_grad = dot(jnp.concatenate([vb, vb], 1), jnp.concatenate([after_hi, after_lo], 0))
-        tail = to_end[:, part]
-        key_out[:, out] = (key[:, part] + tail * from_grad).astype(BF16)
-        key_hi, key_lo = split(k[:, at].astype(F32) * tail)
-        wide = dot(key_hi, jnp.concatenate([after_hi, after_lo], 0), (1, 1))
-        from_key = wide[:, :LANES] + wide[:, LANES:] + dot(key_lo, after_hi, (1, 1))
-        val_out[:, out] = (val[:, part] + from_key).astype(BF16)
+
+    @pl.when(is_first)
+    def _():
+        writer = Writer(group, held, (rec_out,), sems)
+        for pair in range(pairs):
+            (rec, _, _, from_start, _), part = partial_of(pair, early, late)
+            at = slice(pair * LANES, (pair + 1) * LANES)
+            from_state = state_part(dy[:, at], init[:, at])
+            writer.put(pair, rec[:, part] + from_start[:, part] * from_state)
+        writer.finish()
+
+    @pl.when(jnp.logical_not(is_first))
+    def _():
+        writer = Writer(group, held, (key_out, val_out), sems)
+        for pair in range(pairs):
+            (_, key, val, _, _), part = partial_of(pair, early, late)
+            writer.put(pair, key[:, part], val[:, part])
+        writer.finish()
+
+
+def swapped_kernel(group, k, v, dy, swapped, *refs):
+    early, late, outs = refs[:5], refs[5:10], refs[-5:]
+    rec_out, key_out, val_out, held, sems = outs
+    pairs = dy.shape[1] // LANES
+    is_first = lax.axis_index("seq") == 0
+
+    @pl.when(is_first)
+    def _():
+        writer = Writer(group, held, (key_out, val_out), sems)
+        for pair in range(pairs):
+            (_, key, val, _, to_end), part = partial_of(pair, early, late)
+            at = slice(pair * LANES, (pair + 1) * LANES)
+            tail = to_end[:, part]
+            from_grad = state_part(v[:, at], swapped[pair])
+            from_key = key_part(k[:, at].astype(F32) * tail, swapped[pair])
+            writer.put(pair, key[:, part] + tail * from_grad, val[:, part] + from_key)
+        writer.finish()
+
+    @pl.when(jnp.logical_not(is_first))
+    def _():
+        writer = Writer(group, held, (rec_out,), sems)
+        for pair in range(pairs):
+            (rec, _, _, from_start, _), part = partial_of(pair, early, late)
+            at = slice(pair * LANES, (pair + 1) * LANES)
+            from_state = state_part(dy[:, at], swapped[pair])
+            writer.put(pair, rec[:, part] + from_start[:, part] * from_state)
+        writer.finish()
 
 
 def share_kernel(blocks, sent, kept, got, mine, theirs):
@@ -301,6 +374,7 @@
     _, feature = boost.shape
     pairs = width // LANES
     group = 4 if pairs % 4 == 0 else 1
+    state_group = 2 * group if pairs % (2 * group) == 0 else group
     half = feature // 2
     fast = (
         batch == 1
@@ -340,11 +414,11 @@
             )
         operands = (r[b], k[b], v[b], f[b], dy[b], init_t)
         outs = pl.pallas_call(
-            lambda *refs: state_kernel(group, fast, *refs),
+            lambda *refs: state_kernel(state_group, fast, *refs),
             in_specs=[anywhere] * 6,
             out_specs=(vmem,) * 9,
             out_shape=tuple(like(x.shape, x.dtype) for x in operands) + shapes,
-            scratch_shapes=[pltpu.SemaphoreType.DMA((pairs // group, 6))],
+            scratch_shapes=[pltpu.SemaphoreType.DMA((pairs // state_group, 6))],
             compiler_params=limit(24),
             name="states",
             cost_estimate=pl.CostEstimate(
@@ -369,30 +443,38 @@
             ),
         )(*near[:5], boost)
 
-    def outer(near, partial, carried, first=0, count=pairs, prior=()):
+    def outer(near, partial, start, after):
         rec, key, val, from_start, to_end = partial
-        _, k, v, _, dy, start = near
-        group = 4 if count % 4 == 0 else 1
-        block = group * LANES
-
-        def body(*refs):
-            given = 9 + len(carried)
-            outer_kernel(first, group, fast, *refs[:given], *refs[given + len(prior) :])
-
-        here = pl.BlockSpec((toks, block), lambda i: (0, i + first // group))
+        _, k, v, _, dy, _ = near
+        here = pl.BlockSpec((toks, group * LANES), lambda i: (0, i))
+        per_pair = pl.BlockSpec((group, feature, LANES), lambda i: (i, 0, 0))
         return pl.pallas_call(
-            body,
-            grid=(count // group,),
-            in_specs=[vmem] * (9 + len(carried)) + [anywhere] * len(prior),
+            lambda *refs: outer_kernel(group, *refs),
+            grid=(pairs // group,),
+            in_specs=[here] * 8 + [per_pair] * 2,
             out_specs=(here,) * 3,
             out_shape=(like((toks, width), BF16),) * 3,
-            input_output_aliases={9 + len(carried) + i: i for i in range(len(prior))},
             compiler_params=limit(24),
             name="outer",
+        )(k, v, dy, from_start, to_end, rec, key, val, start, after)
+
+    def finish(kernel, operands, prior=()):
+        count = len(operands)
+        return pl.pallas_call(
+            lambda *refs: kernel(group, *refs[:count], *refs[count + len(prior) :]),
+            in_specs=[vmem] * count + [anywhere] * len(prior),
+            out_specs=(anywhere,) * 3,
+            out_shape=(like((toks, width), BF16),) * 3,
+            scratch_shapes=[
+                pltpu.VMEM((2, toks, width), BF16),
+                pltpu.SemaphoreType.DMA((pairs // group, 2)),
+            ],
+            input_output_aliases={count + i: i for i in range(len(prior))},
+            compiler_params=limit(24),
             cost_estimate=pl.CostEstimate(
                 flops=3 * 10**9, bytes_accessed=9 * 2**20, transcendentals=0
             ),
-        )(k, v, dy, from_start, to_end, rec, key, val, start, *carried, *prior)
+        )(*operands, *prior)
 
     def share(sent, kept, got):
         shape = like((pairs // 2, half, LANES))
@@ -434,8 +516,12 @@
             mine, theirs = halve(bit, mine, got)
         total = mine + got
         state_grad = total.transpose(0, 2, 1).reshape(-1, half)
-        results = outer(near, partial_a, (other,), 0, cut)
-        rec, key, val = outer(near, partial_b, (other,), cut, pairs - cut, results)
+        _, k_near, v_near, _, dy_near, init_near = near
+        partial = (*partial_a, *partial_b)
+        results = finish(known_kernel, (dy_near, init_near, *partial))
+        rec, key, val = finish(
+            swapped_kernel, (k_near, v_near, dy_near, other, *partial), results
+        )
         return rec[None], key[None], val[None], state_grad
 
     forward = [(i, i + 1) for i in range(seq_size - 1)]
@@ -450,7 +536,7 @@
             end = whole * start + state_local
             start = jnp.where(is_first, start_t, lax.ppermute(end, "seq", forward))
             after = lax.ppermute(grad_local + whole * after, "seq", backward)
-        results.append(outer(near, inner(near), (start, after)))
+        results.append(outer(near, inner(near), start, after))
         term = term + jnp.where(is_first, grad_local + whole * after, 0.0)
     term = term.transpose(0, 2, 1).reshape(width, feature)
     summed = lax.psum_scatter(term, "dp", scatter_dimension=0, tiled=True)

time: 39.1 us -> 36.4 us (0.931)
  Pallas kernels: 17.6 us -> 16.3 us
  waiting for transfers between devices: 9 us -> 7.82 us
    pallas_call x3, Pallas kernels: 7.42 us -> 6.14 us  [the longest x1 3.27 us: states(): pl.pallas_call(lambda *refs: state_kernel(state_group, fast, *refs), in_s...]
    ppermute x4, waiting for transfers between devices: 2.34 us -> 1.16 us  [on_device(): got = lax.ppermute(theirs, 'dp', [(i, i ^ bit) for i in range(dp_size)])]
    ppermute x4, starting transfers between devices: 6.45 us -> 5.95 us  [on_device(): got = lax.ppermute(theirs, 'dp', [(i, i ^ bit) for i in range(dp_size)])]
  transfers between devices with their start and end apart: 6 -> 6, of which waited for: 3 -> 3; matrix products, arithmetic and copies ran while one was open for 2% -> 2% of each run, Pallas kernels for 26% -> 31%
where the time goes in v2:
time: 36.4 us; the launch traced here: 36.3 us
  Pallas kernels  16.3 us (45%)
  starting transfers between devices  10.8 us (30%)
  waiting for transfers between devices  7.82 us (21%)
  between operations  0.71 us (2%)
  other arithmetic  0.61 us (2%)
    pallas_call x2, Pallas kernels, inner(): pl.pallas_call(body, in_specs=[vmem] * 6, out_specs=(vmem,) * 5, out_shap...  10.1 us
    ppermute x1, waiting for transfers between devices, on_device(): got = lax.ppermute(sent, 'seq', swap)  6.66 us
    ppermute x4, starting transfers between devices, on_device(): got = lax.ppermute(theirs, 'dp', [(i, i ^ bit) for i in range(dp_size)])  5.95 us
    pallas_call x1, Pallas kernels, states(): pl.pallas_call(lambda *refs: state_kernel(state_group, fast, *refs), in_s...  3.27 us
    ppermute x1, starting transfers between devices, on_device(): got = lax.ppermute(sent, 'seq', swap)  3.03 us
    pallas_call x2, Pallas kernels, finish(): pl.pallas_call(lambda *refs: kernel(group, *refs[:count], *refs[count + l...  2.87 us
    ppermute x1, starting transfers between devices, on_device(): other = lax.ppermute(swapped, 'seq', swap)  1.81 us
    ppermute x4, waiting for transfers between devices, on_device(): got = lax.ppermute(theirs, 'dp', [(i, i ^ bit) for i in range(dp_size)])  1.16 us
  transfers between devices with their start and end apart: 6, of which 3 were waited for; matrix products, arithmetic and copies ran while one was open for 2% of the time, Pallas kernels for 31%

profile of v2, /device:TPU:0, one launch (start us, length us, event | category | flops | bytes accessed | tf_op | source)
XLA Modules:
  0.0 36.3 jit_solution(5179705190033197011)
XLA Ops:
  0.6 3.3 %states.1 = (bf16[128,2048]{1,0:T(8,128)(2,1)S(1)}, bf16[128,2048]{1,0:T(8,128)(2,1)S(1)}, bf16[128,2048]{1,0:T(8,128)(2,1)S(1)}, bf16[128,2048]{1,0:T(8,128)(2,...) custom-call(bf16[128,2048]{1,0:T(8,128)(2,1)} %bitcast.13, ...), custom_call_target="tpu_custom_call" | custom-call | flops 4000000000 | bytes 4194304 | tf_op jit(solution)/shard_map/states/pallas_call | solution.py:416
  3.9 3.0 %collective-permute-start.1 = (f32[17,32,128]{2,1,0:T(8,128)S(1)}, f32[17,32,128]{2,1,0:T(8,128)S(1)}, u32[]{:S(2)}, u32[]{:S(2)}) collective-permute-start(f32[17,32,128]{2,1,0:T(8,128)S(1)} %get-tuple-element.60.refs_0_), channel_id=1, source_target_pairs={{0,16},{16,0},{1,17},{17,1},{2,18},{18,2},{3,19},{19,3},{4,20},{20... | collective-permute-start | bytes 835592 | tf_op jit(solution)/shard_map/ppermute | solution.py:504
  6.9 6.7 %collective-permute-done.1.refs_2_ = f32[17,32,128]{2,1,0:T(8,128)S(1)} collective-permute-done((f32[17,32,128]{2,1,0:T(8,128)S(1)}, f32[17,32,128]{2,1,0:T(8,128)S(1)}, u32[]{:S(2)}, u32[]{:S(2)}) %collective-permute-start.1) | collective-permute-done | bytes 278560 | tf_op jit(solution)/shard_map/ppermute | solution.py:504
  13.6 0.1 collective-permute-start.2
  13.7 1.8 %collective-permute-start = (f32[16,64,128]{2,1,0:T(8,128)S(1)}, f32[16,64,128]{2,1,0:T(8,128)S(1)}, u32[]{:S(2)}, u32[]{:S(2)}) collective-permute-start(f32[16,64,128]{2,1,0:T(8,128)S(1)} %get-tuple-element.40), channel_id=1, source_target_pairs={{0,16},{16,0},{1,17},{17,1},{2,18},{18,2},{3,19},{19,3},{4,20},{20... | collective-permute-start | bytes 1572872 | tf_op jit(solution)/shard_map/ppermute | solution.py:505
  15.5 0.0 collective-permute-done.2.refs_1_
  15.5 0.0 copy-start
  15.6 1.6 %collective-permute-start.3 = (f32[4,32,128]{2,1,0:T(8,128)S(1)}, f32[4,32,128]{2,1,0:T(8,128)S(1)}, u32[]{:S(2)}, u32[]{:S(2)}) collective-permute-start(f32[4,32,128]{2,1,0:T(8,128)S(1)} %get-tuple-element.65), channel_id=1, source_target_pairs={{0,2},{1,3},{2,0},{3,1},{4,6},{5,7},{6,4},{7,5},{8,10},{9,11},{10,... | collective-permute-start | bytes 196616 | tf_op jit(solution)/shard_map/ppermute | solution.py:512
  17.1 0.0 copy-done
  17.1 2.5 %inner.3 = (f32[128,512]{1,0:T(8,128)S(1)}, f32[128,512]{1,0:T(8,128)S(1)}, f32[128,512]{1,0:T(8,128)S(1)}, f32[128,512]{1,0:T(8,128)S(1)}, f32[128,512]{1,0:T(8,128)S(1)}) custom-call(bf16[128,2048]{1,0:T(8,128)(2,1)S(1)} %get-tuple-element.41.refs_0_, bf16[128,2048]{1,0:T(8,128)(2,1)S(1)} %get-tuple-element.37.refs_1_.refs_0_, ...), custom_call_target="tpu_custom_call" | custom-call | flops 10000000000 | bytes 8388608 | tf_op jit(solution)/shard_map/inner/pallas_call | solution.py:434
  19.7 0.2 collective-permute-done.3.refs_1_
  19.9 1.6 %collective-permute-start.4 = (f32[2,32,128]{2,1,0:T(8,128)S(1)}, f32[2,32,128]{2,1,0:T(8,128)S(1)}, u32[]{:S(2)}, u32[]{:S(2)}) collective-permute-start(f32[2,32,128]{2,1,0:T(8,128)S(1)} %get-tuple-element.67), channel_id=1, source_target_pairs={{0,4},{1,5},{2,6},{3,7},{4,0},{5,1},{6,2},{7,3},{8,12},{9,13},{10,... | collective-permute-start | bytes 98312 | tf_op jit(solution)/shard_map/ppermute | solution.py:512
  21.5 7.6 %inner.2 = (f32[128,1536]{1,0:T(8,128)S(1)}, f32[128,1536]{1,0:T(8,128)S(1)}, f32[128,1536]{1,0:T(8,128)S(1)}, f32[128,1536]{1,0:T(8,128)S(1)}, f32[128,1536]{1,0:T(8,128)S(1)}) custom-call(bf16[128,2048]{1,0:T(8,128)(2,1)S(1)} %get-tuple-element.41.refs_0_, bf16[128,2048]{1,0:T(8,128)(2,1)S(1)} %get-tuple-element.37.refs_1_.refs_0_, ...), custom_call_target="tpu_custom_call" | custom-call | flops 10000000000 | bytes 8388608 | tf_op jit(solution)/shard_map/inner/pallas_call | solution.py:434
  29.1 0.0 collective-permute-done.4.refs_1_
  29.2 2.7 %collective-permute-start.5 = (f32[1,32,128]{2,1,0:T(8,128)S(1)}, f32[1,32,128]{2,1,0:T(8,128)S(1)}, u32[]{:S(2)}, u32[]{:S(2)}) collective-permute-start(f32[1,32,128]{2,1,0:T(8,128)S(1)} %get-tuple-element.69), channel_id=1, source_target_pairs={{0,8},{1,9},{2,10},{3,11},{4,12},{5,13},{6,14},{7,15},{8,0},{9,1},... | collective-permute-start | bytes 49160 | tf_op jit(solution)/shard_map/ppermute | solution.py:512
  31.8 1.2 %shard_map.102 = (bf16[128,2048]{1,0:T(8,128)(2,1)}, bf16[128,2048]{1,0:T(8,128)(2,1)}, bf16[128,2048]{1,0:T(8,128)(2,1)}) custom-call(bf16[128,2048]{1,0:T(8,128)(2,1)S(1)} %get-tuple-element.39.refs_4_.refs_0_.refs_2_, f32[64,2048]{1,0:T(8,128)S(1)} %get-tuple-element.53.refs_1_, f32[128,1536]{1,0:T(8,128)S(1)} %get-tuple-element.43.refs_2_.refs_4_, ...), custom_call_target="tpu_custom_call" | custom-call | flops 3000000000 | bytes 9437184 | tf_op jit(solution)/shard_map/pallas_call | solution.py:463
  33.0 0.9 %collective-permute-done.5 = f32[1,32,128]{2,1,0:T(8,128)S(1)} collective-permute-done((f32[1,32,128]{2,1,0:T(8,128)S(1)}, f32[1,32,128]{2,1,0:T(8,128)S(1)}, u32[]{:S(2)}, u32[]{:S(2)}) %collective-permute-start.5) | collective-permute-done | bytes 16416 | tf_op jit(solution)/shard_map/ppermute | solution.py:512
  34.0 0.6 %add_bitcast_fusion = f32[128,32]{0,1:T(8,128)} fusion(f32[1,32,128]{2,1,0:T(8,128)S(1)} %get-tuple-element.68, f32[1,32,128]{2,1,0:T(8,128)S(1)} %collective-permute-done.5), kind=kLoop, calls=%fused_computation | loop fusion | flops 4096 | bytes 49152 | tf_op jit(solution)/shard_map/reshape | solution.py:518
  34.6 0.0 collective-permute-done.refs_3_
  34.6 1.7 %shard_map.103 = (bf16[128,2048]{1,0:T(8,128)(2,1)}, bf16[128,2048]{1,0:T(8,128)(2,1)}, bf16[128,2048]{1,0:T(8,128)(2,1)}) custom-call(bf16[128,2048]{1,0:T(8,128)(2,1)S(1)} %get-tuple-element.37.refs_1_.refs_0_, bf16[128,2048]{1,0:T(8,128)(2,1)S(1)} %get-tuple-element.38.refs_2_.refs_1_, ...), custom_call_target="tpu_custom_call", output_to_operand_aliasing={{0}: (14, {}), {1}: (15, {}), {2}: (16, {})} | custom-call | flops 3000000000 | bytes 9437184 | tf_op jit(solution)/shard_map/pallas_call | solution.py:463
  (4 shorter events, 0.1 us)
Async XLA Ops:
  3.9 9.7 %collective-permute-start.1 = (f32[17,32,128]{2,1,0:T(8,128)S(1)}, f32[17,32,128]{2,1,0:T(8,128)S(1)}, u32[]{:S(2)}, u32[]{:S(2)}) collective-permute-start(f32[17,32,128]{2,1,0:T(8,128)S(1)} %get-tuple-element.60.refs_0_), channel_id=1, source_target_pairs={{0,16},{16,0},{1,17},{17,1},{2,18},{18,2},{3,19},{19,3},{4,20},{20... | collective-permute-start | bytes 835592 | tf_op jit(solution)/shard_map/ppermute | solution.py:504
  13.6 1.9 %collective-permute-start.2 = (f32[8,32,128]{2,1,0:T(8,128)S(1)}, f32[8,32,128]{2,1,0:T(8,128)S(1)}, u32[]{:S(2)}, u32[]{:S(2)}) collective-permute-start(f32[8,32,128]{2,1,0:T(8,128)S(1)} %get-tuple-element.63), channel_id=1, source_target_pairs={{0,1},{1,0},{2,3},{3,2},{4,5},{5,4},{6,7},{7,6},{8,9},{9,8},{10,11... | collective-permute-start | bytes 393224 | tf_op jit(solution)/shard_map/ppermute | solution.py:512
  13.7 20.8 %collective-permute-start = (f32[16,64,128]{2,1,0:T(8,128)S(1)}, f32[16,64,128]{2,1,0:T(8,128)S(1)}, u32[]{:S(2)}, u32[]{:S(2)}) collective-permute-start(f32[16,64,128]{2,1,0:T(8,128)S(1)} %get-tuple-element.40), channel_id=1, source_target_pairs={{0,16},{16,0},{1,17},{17,1},{2,18},{18,2},{3,19},{19,3},{4,20},{20... | collective-permute-start | bytes 1572872 | tf_op jit(solution)/shard_map/ppermute | solution.py:505
  15.5 1.6 %copy-start = (f32[32,64]{1,0:T(8,128)S(1)}, f32[32,64]{1,0:T(8,128)}, u32[]{:S(2)}) copy-start(f32[32,64]{1,0:T(8,128)} %refs_5_.3) | copy-start | bytes 24580
  15.6 4.3 %collective-permute-start.3 = (f32[4,32,128]{2,1,0:T(8,128)S(1)}, f32[4,32,128]{2,1,0:T(8,128)S(1)}, u32[]{:S(2)}, u32[]{:S(2)}) collective-permute-start(f32[4,32,128]{2,1,0:T(8,128)S(1)} %get-tuple-element.65), channel_id=1, source_target_pairs={{0,2},{1,3},{2,0},{3,1},{4,6},{5,7},{6,4},{7,5},{8,10},{9,11},{10,... | collective-permute-start | bytes 196616 | tf_op jit(solution)/shard_map/ppermute | solution.py:512
  19.9 9.3 %collective-permute-start.4 = (f32[2,32,128]{2,1,0:T(8,128)S(1)}, f32[2,32,128]{2,1,0:T(8,128)S(1)}, u32[]{:S(2)}, u32[]{:S(2)}) collective-permute-start(f32[2,32,128]{2,1,0:T(8,128)S(1)} %get-tuple-element.67), channel_id=1, source_target_pairs={{0,4},{1,5},{2,6},{3,7},{4,0},{5,1},{6,2},{7,3},{8,12},{9,13},{10,... | collective-permute-start | bytes 98312 | tf_op jit(solution)/shard_map/ppermute | solution.py:512
  29.2 4.8 %collective-permute-start.5 = (f32[1,32,128]{2,1,0:T(8,128)S(1)}, f32[1,32,128]{2,1,0:T(8,128)S(1)}, u32[]{:S(2)}, u32[]{:S(2)}) collective-permute-start(f32[1,32,128]{2,1,0:T(8,128)S(1)} %get-tuple-element.69), channel_id=1, source_target_pairs={{0,8},{1,9},{2,10},{3,11},{4,12},{5,13},{6,14},{7,15},{8,0},{9,1},... | collective-permute-start | bytes 49160 | tf_op jit(solution)/shard_map/ppermute | solution.py:512

commit v3 on v2

--- a/solution.py
+++ b/solution.py
@@ -24,44 +24,49 @@
     return hi, (x - hi.astype(F32)).astype(BF16)
 
 
-def triangles(toks):
+def interleave(works):
+    works = list(works)
+    while works:
+        works = [w for w in works if next(w, works) is not works]
+
+
+def triangle(toks, after):
     row = lax.broadcasted_iota(jnp.int32, (toks, toks), 0)
     col = lax.broadcasted_iota(jnp.int32, (toks, toks), 1)
     same = (row // CHUNK) == (col // CHUNK)
-    before = jnp.where(same & (col < row), 1.0, 0.0).astype(BF16)
-    after = jnp.where(same & (col > row), 1.0, 0.0).astype(BF16)
-    return jnp.concatenate([before, after], 0)
-
-
-def decays(fade, tri):
-    toks = fade.shape[0]
-    log_decay = -jnp.exp(fade.astype(F32))
+    order = (col > row) if after else (col < row)
+    return jnp.where(same & order, 1.0, 0.0).astype(BF16)
+
+
+def log_sums(log_decay, *tris):
     hi, lo = split(log_decay)
+    tri = jnp.concatenate(tris, 0)
     sums = dot(jnp.concatenate([tri, tri], 1), jnp.concatenate([hi, lo], 0))
-    prefix, suffix = sums[:toks], sums[toks:]
-    totals, middles = [], []
-    for c in range(toks // CHUNK):
-        last = (c + 1) * CHUNK - 1
-        totals.append(prefix[last : last + 1] + log_decay[last : last + 1])
-        mid = c * CHUNK + CHUNK // 2
-        middles.append(prefix[mid : mid + 1])
-    return jnp.exp(prefix), jnp.exp(suffix), totals, middles
-
-
-def spread(early, late, totals):
+    toks = log_decay.shape[0]
+    return [sums[i * toks : (i + 1) * toks] for i in range(len(tris))]
+
+
+def log_decay_of(fade):
+    return -jnp.exp(fade.astype(F32))
+
+
+def chunk_totals(sums, log_decay, after):
+    totals = []
+    for c in range(log_decay.shape[0] // CHUNK):
+        at = c * CHUNK if after else (c + 1) * CHUNK - 1
+        totals.append(sums[at : at + 1] + log_decay[at : at + 1])
+    return totals
+
+
+def spread(factors, totals, after):
     chunks = len(totals)
-    rows = [slice(c * CHUNK, (c + 1) * CHUNK) for c in range(chunks)]
-    from_start, to_end = [], []
+    order = range(chunks)[::-1] if after else range(chunks)
+    pieces = [None] * chunks
     run = jnp.zeros_like(totals[0])
-    for c in range(chunks):
-        from_start.append(early[rows[c]] * jnp.exp(run))
+    for c in order:
+        pieces[c] = factors[c * CHUNK : (c + 1) * CHUNK] * jnp.exp(run)
         run = run + totals[c]
-    whole = jnp.exp(run)
-    run = jnp.zeros_like(totals[0])
-    for c in reversed(range(chunks)):
-        to_end.append(late[rows[c]] * jnp.exp(run))
-        run = run + totals[c]
-    return jnp.concatenate(from_start, 0), jnp.concatenate(to_end[::-1], 0), whole
+    return jnp.concatenate(pieces, 0), jnp.exp(run)
 
 
 def first_head(shape):
@@ -79,11 +84,11 @@
     return jnp.where(first_head((half, LANES)), x[:half], x[half:])
 
 
-def state_kernel(group, fast, *refs):
+def grad_kernel(group, fast, *refs):
     sources, refs = refs[:6], refs[6:]
     copies, refs = refs[:6], refs[6:]
-    outs, sems = refs[:-1], refs[-1]
-    r, k, v, f, dy, init = copies
+    (from_out, *outs), sems = refs[:-1], refs[-1]
+    f, r, dy = copies[:3]
     toks, width = r.shape
     steps = width // LANES // group
     is_first = lax.axis_index("seq") == 0
@@ -94,37 +99,71 @@
             sources[i].at[:, lanes], copies[i].at[:, lanes], sems.at[step, i]
         )
 
-    order = (3, 0, 4, 1, 2, 5)
+    for part in (range(3), range(3, 6)):
+        for step in range(steps):
+            for i in part:
+                fetch(step, i).start()
+    tri = triangle(toks, False)
+
+    def work(pair):
+        at = slice(pair * LANES, (pair + 1) * LANES)
+        log_decay = log_decay_of(f[:, at])
+        (before,) = log_sums(log_decay, tri)
+        yield
+        totals = chunk_totals(before, log_decay, False)
+        from_start, whole = spread(jnp.exp(before), totals, False)
+        from_out[:, at] = from_start
+        rec_hi, rec_lo = split(r[:, at].astype(F32) * from_start)
+        grad = dot(dy[:, at], jnp.concatenate([rec_hi, rec_lo], 1), (0, 0))
+        yield
+        grad = diagonal(grad[:, :LANES] + grad[:, LANES:])
+        if fast:
+            sent, kept = outs
+            half = grad.shape[0] // 2
+            sent[pair] = jnp.where(is_first, grad[half:], grad[:half])
+            kept[pair] = jnp.where(is_first, grad[:half], grad[half:])
+            sent[sent.shape[0] - 1, pair : pair + 1] = whole
+        else:
+            grads, wholes = outs
+            grads[pair] = grad
+            wholes[pair] = whole
+
     for step in range(steps):
-        for i in order:
-            fetch(step, i).start()
-    tri = triangles(toks)
+        for i in range(3):
+            fetch(step, i).wait()
+        interleave(work(step * group + p) for p in range(group))
     for step in range(steps):
-        for i in order:
+        for i in range(3, 6):
             fetch(step, i).wait()
-        for pair in range(step * group, (step + 1) * group):
-            at = slice(pair * LANES, (pair + 1) * LANES)
-            early, late, totals, _ = decays(f[:, at], tri)
-            from_start, to_end, whole = spread(early, late, totals)
-            key_hi, key_lo = split(k[:, at].astype(F32) * to_end)
-            rec_hi, rec_lo = split(r[:, at].astype(F32) * from_start)
-            state = dot(v[:, at], jnp.concatenate([key_hi, key_lo], 1), (0, 0))
-            grad = dot(dy[:, at], jnp.concatenate([rec_hi, rec_lo], 1), (0, 0))
-            state = diagonal(state[:, :LANES] + state[:, LANES:])
-            grad = diagonal(grad[:, :LANES] + grad[:, LANES:])
-            if fast:
-                sent, kept, swapped = outs
-                half = grad.shape[0] // 2
-                end = whole * init[:, at] + state
-                swapped[pair] = jnp.where(is_first, end, grad)
-                sent[pair] = jnp.where(is_first, grad[half:], grad[:half])
-                kept[pair] = jnp.where(is_first, grad[:half], grad[half:])
-                sent[sent.shape[0] - 1, pair : pair + 1] = whole
-            else:
-                states, grads, wholes = outs
-                states[pair] = state
-                grads[pair] = grad
-                wholes[pair] = whole
+
+
+def end_kernel(group, fast, f, k, v, init, *refs):
+    to_out, state_out = refs[-2:]
+    toks, width = k.shape
+    tri = triangle(toks, True)
+    is_first = lax.axis_index("seq") == 0
+
+    def work(pair):
+        at = slice(pair * LANES, (pair + 1) * LANES)
+        log_decay = log_decay_of(f[:, at])
+        (behind,) = log_sums(log_decay, tri)
+        yield
+        totals = chunk_totals(behind, log_decay, True)
+        to_end, whole = spread(jnp.exp(behind), totals, True)
+        to_out[:, at] = to_end
+        key_hi, key_lo = split(k[:, at].astype(F32) * to_end)
+        state = dot(v[:, at], jnp.concatenate([key_hi, key_lo], 1), (0, 0))
+        yield
+        state = diagonal(state[:, :LANES] + state[:, LANES:])
+        if fast:
+            sent, kept = refs[:2]
+            grad = jnp.concatenate([sent[pair], kept[pair]], 0)
+            state_out[pair] = jnp.where(is_first, whole * init[:, at] + state, grad)
+        else:
+            state_out[pair] = state
+
+    for step in range(width // LANES // group):
+        interleave(work(step * group + p) for p in range(group))
 
 
 def inner_kernel(first, count, unroll, r, k, v, f, dy, boost, *outs):
@@ -136,10 +175,10 @@
     lax.fori_loop(0, count // unroll, step, 0)
 
 
-def inner_pairs(base, out_base, pairs, r, k, v, f, dy, boost, rec, key, val, from_out, to_out):
+def inner_pairs(base, out_base, pairs, r, k, v, f, dy, boost, rec, key, val):
     toks = r.shape[0]
     chunks = toks // CHUNK
-    tri = triangles(toks)
+    tris = triangle(toks, False), triangle(toks, True)
     keep = first_head((toks, LANES))
     keep_chunk = first_head((CHUNK, LANES))
     row = lax.broadcasted_iota(jnp.int32, (CHUNK, CHUNK), 0)
@@ -156,13 +195,16 @@
         )
 
     rows = [slice(c * CHUNK, (c + 1) * CHUNK) for c in range(chunks)]
-    for p in range(pairs):
+
+    def work(p):
         at = pl.ds(pl.multiple_of(base + p * LANES, LANES), LANES)
         to = pl.ds(pl.multiple_of(out_base + p * LANES, LANES), LANES)
-        early, late, totals, middles = decays(f[:, at], tri)
-        from_start, to_end, _ = spread(early, late, totals)
-        from_out[:, to] = from_start
-        to_out[:, to] = to_end
+        log_decay = log_decay_of(f[:, at])
+        before, behind = log_sums(log_decay, *tris)
+        totals = chunk_totals(before, log_decay, False)
+        mids = [c * CHUNK + CHUNK // 2 for c in range(chunks)]
+        middles = [before[mid : mid + 1] for mid in mids]
+        early, late = jnp.exp(before), jnp.exp(behind)
         rb, kb, vb, db = r[:, at], k[:, at], v[:, at], dy[:, at]
         rf, kf, vf, df = (x.astype(F32) for x in (rb, kb, vb, db))
         head = 2 * (base // LANES + p)
@@ -171,13 +213,14 @@
         key_late = kf * late
         dy_heads = by_head(flip(db))
         scores = dot(db, by_head(vb), (1, 1))
-        scores_t = dot(vb, dy_heads, (1, 1))
         scores_split, scores_t_split = [], []
         for h in range(2):
             part = slice(h * toks, (h + 1) * toks)
-            scores_split.append(split(jnp.where(below, scores[:, part], 0.0)))
-            scores_t_split.append(split(jnp.where(above, scores_t[:, part], 0.0)))
+            halves = split(jnp.where(below, scores[:, part], 0.0))
+            scores_split.append(halves)
+            scores_t_split.append([flip(x).T for x in halves])
         rec_rows, key_rows, cross_rows = [], [], []
+        yield
         for c in range(chunks):
             here = rows[c]
             count = (c + 1) * CHUNK
@@ -223,6 +266,7 @@
             cross_rows.append(
                 [jnp.where(above[here], got[h * CHUNK : (h + 1) * CHUNK], 0.0) for h in range(2)]
             )
+            yield
         cross = jnp.concatenate(
             [jnp.concatenate([c[h] for c in cross_rows], 0) for h in range(2)], 1
         )
@@ -240,6 +284,8 @@
         rec[:, to] = jnp.concatenate(rec_rows, 0) + kf * boosted
         key[:, to] = jnp.concatenate(key_rows, 0) + rf * boosted
         val[:, to] = inner_val + head_sum(mix) * df
+
+    interleave(work(p) for p in range(pairs))
 
 
 def state_part(rows, state):
@@ -297,57 +343,72 @@
     return refs, slice(place * LANES, (place + 1) * LANES)
 
 
-def known_kernel(group, dy, init, *refs):
-    early, late, (rec_out, key_out, val_out, held, sems) = refs[:5], refs[5:10], refs[10:]
-    pairs = dy.shape[1] // LANES
+def by_groups(group, pairs, work):
+    for first in range(0, pairs, group):
+        interleave(work(pair) for pair in range(first, first + group))
+
+
+def rec_writer(group, dy, from_start, state_of, early, late, out, held, sems):
+    writer = Writer(group, held, (out,), sems)
+
+    def work(pair):
+        rec, part = partial_of(pair, early, late)
+        at = slice(pair * LANES, (pair + 1) * LANES)
+        from_state = state_part(dy[:, at], state_of(pair))
+        yield
+        writer.put(pair, rec[0][:, part] + from_start[:, at] * from_state)
+
+    by_groups(group, dy.shape[1] // LANES, work)
+    writer.finish()
+
+
+def known_kernel(group, dy, init, from_start, *refs):
+    early, late, (rec_out, key_out, val_out, held, sems) = refs[:3], refs[3:6], refs[6:]
     is_first = lax.axis_index("seq") == 0
 
     @pl.when(is_first)
     def _():
-        writer = Writer(group, held, (rec_out,), sems)
-        for pair in range(pairs):
-            (rec, _, _, from_start, _), part = partial_of(pair, early, late)
-            at = slice(pair * LANES, (pair + 1) * LANES)
-            from_state = state_part(dy[:, at], init[:, at])
-            writer.put(pair, rec[:, part] + from_start[:, part] * from_state)
-        writer.finish()
+        def state_of(pair):
+            return init[:, pair * LANES : (pair + 1) * LANES]
+
+        rec_writer(group, dy, from_start, state_of, early, late, rec_out, held, sems)
 
     @pl.when(jnp.logical_not(is_first))
     def _():
         writer = Writer(group, held, (key_out, val_out), sems)
-        for pair in range(pairs):
-            (_, key, val, _, _), part = partial_of(pair, early, late)
+        for pair in range(dy.shape[1] // LANES):
+            (_, key, val), part = partial_of(pair, early, late)
             writer.put(pair, key[:, part], val[:, part])
         writer.finish()
 
 
-def swapped_kernel(group, k, v, dy, swapped, *refs):
-    early, late, outs = refs[:5], refs[5:10], refs[-5:]
+def swapped_kernel(group, k, v, dy, swapped, from_start, to_end, *refs):
+    early, late, outs = refs[:3], refs[3:6], refs[-5:]
     rec_out, key_out, val_out, held, sems = outs
-    pairs = dy.shape[1] // LANES
     is_first = lax.axis_index("seq") == 0
 
     @pl.when(is_first)
     def _():
         writer = Writer(group, held, (key_out, val_out), sems)
-        for pair in range(pairs):
-            (_, key, val, _, to_end), part = partial_of(pair, early, late)
+
+        def work(pair):
+            (_, key, val), part = partial_of(pair, early, late)
             at = slice(pair * LANES, (pair + 1) * LANES)
-            tail = to_end[:, part]
+            tail = to_end[:, at]
             from_grad = state_part(v[:, at], swapped[pair])
             from_key = key_part(k[:, at].astype(F32) * tail, swapped[pair])
+            yield
             writer.put(pair, key[:, part] + tail * from_grad, val[:, part] + from_key)
+
+        by_groups(group, dy.shape[1] // LANES, work)
         writer.finish()
 
     @pl.when(jnp.logical_not(is_first))
     def _():
-        writer = Writer(group, held, (rec_out,), sems)
-        for pair in range(pairs):
-            (rec, _, _, from_start, _), part = partial_of(pair, early, late)
-            at = slice(pair * LANES, (pair + 1) * LANES)
-            from_state = state_part(dy[:, at], swapped[pair])
-            writer.put(pair, rec[:, part] + from_start[:, part] * from_state)
-        writer.finish()
+        def state_of(pair):
+            return swapped[pair]
+
+        rec_writer(group, dy, from_start, state_of, early, late, rec_out, held, sems)
 
 
 def share_kernel(blocks, sent, kept, got, mine, theirs):
@@ -399,33 +460,41 @@
     def in_hbm(x):
         return pltpu.with_memory_space_constraint(x, pltpu.HBM)
 
-    def states(b):
+    def grads(b):
         if fast:
-            shapes = (
-                like((pairs + 1, half, LANES)),
-                like((pairs, half, LANES)),
-                like((pairs, feature, LANES)),
-            )
+            shapes = (like((pairs + 1, half, LANES)), like((pairs, half, LANES)))
         else:
-            shapes = (
-                like((pairs, feature, LANES)),
-                like((pairs, feature, LANES)),
-                like((pairs, 1, LANES)),
-            )
-        operands = (r[b], k[b], v[b], f[b], dy[b], init_t)
+            shapes = (like((pairs, feature, LANES)), like((pairs, 1, LANES)))
+        operands = (f[b], r[b], dy[b], k[b], v[b], init_t)
         outs = pl.pallas_call(
-            lambda *refs: state_kernel(state_group, fast, *refs),
+            lambda *refs: grad_kernel(state_group, fast, *refs),
             in_specs=[anywhere] * 6,
-            out_specs=(vmem,) * 9,
-            out_shape=tuple(like(x.shape, x.dtype) for x in operands) + shapes,
+            out_specs=(vmem,) * (7 + len(shapes)),
+            out_shape=tuple(like(x.shape, x.dtype) for x in operands)
+            + (like((toks, width)),)
+            + shapes,
             scratch_shapes=[pltpu.SemaphoreType.DMA((pairs // state_group, 6))],
             compiler_params=limit(24),
-            name="states",
+            name="grads",
             cost_estimate=pl.CostEstimate(
                 flops=4 * 10**9, bytes_accessed=4 * 2**20, transcendentals=10**6
             ),
         )(*(in_hbm(x) for x in operands))
-        return outs[:6], outs[6:]
+        return outs[:6], outs[6], outs[7:]
+
+    def ends(near, *grad):
+        f, _, _, k, v, init = near
+        return pl.pallas_call(
+            lambda *refs: end_kernel(state_group, fast, *refs),
+            in_specs=[vmem] * (4 + len(grad)),
+            out_specs=(vmem,) * 2,
+            out_shape=(like((toks, width)), like((pairs, feature, LANES))),
+            compiler_params=limit(24),
+            name="ends",
+            cost_estimate=pl.CostEstimate(
+                flops=4 * 10**9, bytes_accessed=4 * 2**20, transcendentals=10**6
+            ),
+        )(f, k, v, init, *grad)
 
     def inner(near, first=0, count=pairs):
         def body(*refs):
@@ -434,18 +503,18 @@
         return pl.pallas_call(
             body,
             in_specs=[vmem] * 6,
-            out_specs=(vmem,) * 5,
-            out_shape=(like((toks, count * LANES)),) * 5,
+            out_specs=(vmem,) * 3,
+            out_shape=(like((toks, count * LANES)),) * 3,
             compiler_params=limit(24),
             name="inner",
             cost_estimate=pl.CostEstimate(
                 flops=10**10, bytes_accessed=8 * 2**20, transcendentals=10**6
             ),
-        )(*near[:5], boost)
-
-    def outer(near, partial, start, after):
-        rec, key, val, from_start, to_end = partial
-        _, k, v, _, dy, _ = near
+        )(near[1], near[3], near[4], near[0], near[2], boost)
+
+    def outer(near, partial, from_start, to_end, start, after):
+        rec, key, val = partial
+        _, _, dy, k, v, _ = near
         here = pl.BlockSpec((toks, group * LANES), lambda i: (0, i))
         per_pair = pl.BlockSpec((group, feature, LANES), lambda i: (i, 0, 0))
         return pl.pallas_call(
@@ -499,9 +568,10 @@
         )(mine, got)
 
     if fast:
-        near, (sent, kept, swapped) = states(0)
+        near, from_start, (sent, kept) = grads(0)
         swap = [(0, 1), (1, 0)]
         got = lax.ppermute(sent, "seq", swap)
+        to_end, swapped = ends(near, sent, kept)
         other = lax.ppermute(swapped, "seq", swap)
         cut = 3 * pairs // 4
         partial_a = inner(near, 0, cut)
@@ -516,11 +586,13 @@
             mine, theirs = halve(bit, mine, got)
         total = mine + got
         state_grad = total.transpose(0, 2, 1).reshape(-1, half)
-        _, k_near, v_near, _, dy_near, init_near = near
+        _, _, dy_near, k_near, v_near, init_near = near
         partial = (*partial_a, *partial_b)
-        results = finish(known_kernel, (dy_near, init_near, *partial))
+        results = finish(known_kernel, (dy_near, init_near, from_start, *partial))
         rec, key, val = finish(
-            swapped_kernel, (k_near, v_near, dy_near, other, *partial), results
+            swapped_kernel,
+            (k_near, v_near, dy_near, other, from_start, to_end, *partial),
+            results,
         )
         return rec[None], key[None], val[None], state_grad
 
@@ -529,14 +601,15 @@
     start_t = init_t.reshape(feature, pairs, LANES).transpose(1, 0, 2)
     results, term = [], 0.0
     for b in range(batch):
-        near, (state_local, grad_local, whole) = states(b)
+        near, from_start, (grad_local, whole) = grads(b)
+        to_end, state_local = ends(near)
         start = start_t
         after = jnp.zeros_like(grad_local)
         for _ in range(seq_size - 1):
             end = whole * start + state_local
             start = jnp.where(is_first, start_t, lax.ppermute(end, "seq", forward))
             after = lax.ppermute(grad_local + whole * after, "seq", backward)
-        results.append(outer(near, inner(near), start, after))
+        results.append(outer(near, inner(near), from_start, to_end, start, after))
         term = term + jnp.where(is_first, grad_local + whole * after, 0.0)
     term = term.transpose(0, 2, 1).reshape(width, feature)
     summed = lax.psum_scatter(term, "dp", scatter_dimension=0, tiled=True)

time: 36.4 us -> 33.8 us (0.929)
  Pallas kernels: 16.3 us -> 12.7 us
  waiting for transfers between devices: 7.82 us -> 8.78 us
    pallas_call x3 -> x4, Pallas kernels: 13.4 us -> 9.75 us  [the longest x2 6.38 us: inner(): pl.pallas_call(body, in_specs=[vmem] * 6, out_specs=(vmem,) * 3, out_shap...]
    ppermute x4, waiting for transfers between devices: 1.16 us -> 2.12 us  [on_device(): got = lax.ppermute(theirs, 'dp', [(i, i ^ bit) for i in range(dp_size)])]
  transfers between devices with their start and end apart: 6 -> 6, of which waited for: 3 -> 3; matrix products, arithmetic and copies ran while one was open for 2% -> 2% of each run, Pallas kernels for 31% -> 26%
where the time goes in v3:
time: 33.8 us; the launch traced here: 33.6 us
  Pallas kernels  12.7 us (38%)
  starting transfers between devices  10.8 us (32%)
  waiting for transfers between devices  8.78 us (26%)
  between operations  0.71 us (2%)
  other arithmetic  0.61 us (2%)
    ppermute x1, waiting for transfers between devices, on_device(): got = lax.ppermute(sent, 'seq', swap)  6.66 us
    pallas_call x2, Pallas kernels, inner(): pl.pallas_call(body, in_specs=[vmem] * 6, out_specs=(vmem,) * 3, out_shap...  6.38 us
    ppermute x4, starting transfers between devices, on_device(): got = lax.ppermute(theirs, 'dp', [(i, i ^ bit) for i in range(dp_size)])  5.95 us
    ppermute x1, starting transfers between devices, on_device(): got = lax.ppermute(sent, 'seq', swap)  3.03 us
    pallas_call x2, Pallas kernels, finish(): pl.pallas_call(lambda *refs: kernel(group, *refs[:count], *refs[count + l...  2.87 us
    pallas_call x1, Pallas kernels, grads(): pl.pallas_call(lambda *refs: grad_kernel(state_group, fast, *refs), in_sp...  2.33 us
    ppermute x4, waiting for transfers between devices, on_device(): got = lax.ppermute(theirs, 'dp', [(i, i ^ bit) for i in range(dp_size)])  2.12 us
    ppermute x1, starting transfers between devices, on_device(): other = lax.ppermute(swapped, 'seq', swap)  1.8 us
  transfers between devices with their start and end apart: 6, of which 3 were waited for; matrix products, arithmetic and copies ran while one was open for 2% of the time, Pallas kernels for 26%

profile of v3, /device:TPU:0, one launch (start us, length us, event | category | flops | bytes accessed | tf_op | source)
XLA Modules:
  0.0 33.6 jit_solution(15246827437183683171)
XLA Ops:
  0.6 2.3 %grads.1 = (bf16[128,2048]{1,0:T(8,128)(2,1)S(1)}, bf16[128,2048]{1,0:T(8,128)(2,1)S(1)}, bf16[128,2048]{1,0:T(8,128)(2,1)S(1)}, bf16[128,2048]{1,0:T(8,128)(2,1...) custom-call(bf16[128,2048]{1,0:T(8,128)(2,1)} %bitcast.13, ...), custom_call_target="tpu_custom_call" | custom-call | flops 4000000000 | bytes 4194304 | tf_op jit(solution)/shard_map/grads/pallas_call | solution.py:469
  3.0 3.0 %collective-permute-start.1 = (f32[17,32,128]{2,1,0:T(8,128)S(1)}, f32[17,32,128]{2,1,0:T(8,128)S(1)}, u32[]{:S(2)}, u32[]{:S(2)}) collective-permute-start(f32[17,32,128]{2,1,0:T(8,128)S(1)} %get-tuple-element.40.refs_4_.refs_0_), channel_id=1, source_target_pairs={{0,16},{16,0},{1,17},{17,1},{2,18},{18,2},{3,19},{19,3},{4,20},{20... | collective-permute-start | bytes 835592 | tf_op jit(solution)/shard_map/ppermute | solution.py:573
  6.0 6.7 %collective-permute-done.1.refs_2_ = f32[17,32,128]{2,1,0:T(8,128)S(1)} collective-permute-done((f32[17,32,128]{2,1,0:T(8,128)S(1)}, f32[17,32,128]{2,1,0:T(8,128)S(1)}, u32[]{:S(2)}, u32[]{:S(2)}) %collective-permute-start.1) | collective-permute-done | bytes 278560 | tf_op jit(solution)/shard_map/ppermute | solution.py:573
  12.7 0.1 collective-permute-start.2
  12.8 1.0 %ends.1 = (f32[128,2048]{1,0:T(8,128)S(1)}, f32[16,64,128]{2,1,0:T(8,128)S(1)}) custom-call(bf16[128,2048]{1,0:T(8,128)(2,1)S(1)} %get-tuple-element.38.refs_0_.refs_3_, bf16[128,2048]{1,0:T(8,128)(2,1)S(1)} %get-tuple-element.35.refs_1_.refs_0_, bf16[128,2048]{1,0:T(8,128)(2,1)S(1)} %get-tuple-element.36.refs_2_.refs_1_, ...), custom_call_target="tpu_custom_call" | custom-call | flops 4000000000 | bytes 4194304 | tf_op jit(solution)/shard_map/ends/pallas_call | solution.py:487
  13.8 1.8 %collective-permute-start = (f32[16,64,128]{2,1,0:T(8,128)S(1)}, f32[16,64,128]{2,1,0:T(8,128)S(1)}, u32[]{:S(2)}, u32[]{:S(2)}) collective-permute-start(f32[16,64,128]{2,1,0:T(8,128)S(1)} %get-tuple-element.42), channel_id=1, source_target_pairs={{0,16},{16,0},{1,17},{17,1},{2,18},{18,2},{3,19},{19,3},{4,20},{20... | collective-permute-start | bytes 1572872 | tf_op jit(solution)/shard_map/ppermute | solution.py:575
  15.6 0.0 collective-permute-done.2.refs_1_
  15.6 0.0 copy-start
  15.7 1.6 %collective-permute-start.3 = (f32[4,32,128]{2,1,0:T(8,128)S(1)}, f32[4,32,128]{2,1,0:T(8,128)S(1)}, u32[]{:S(2)}, u32[]{:S(2)}) collective-permute-start(f32[4,32,128]{2,1,0:T(8,128)S(1)} %get-tuple-element.61), channel_id=1, source_target_pairs={{0,2},{1,3},{2,0},{3,1},{4,6},{5,7},{6,4},{7,5},{8,10},{9,11},{10,... | collective-permute-start | bytes 196616 | tf_op jit(solution)/shard_map/ppermute | solution.py:582
  17.3 0.0 copy-done
  17.3 1.5 %inner.3 = (f32[128,512]{1,0:T(8,128)S(1)}, f32[128,512]{1,0:T(8,128)S(1)}, f32[128,512]{1,0:T(8,128)S(1)}) custom-call(bf16[128,2048]{1,0:T(8,128)(2,1)S(1)} %get-tuple-element.45.refs_0_, bf16[128,2048]{1,0:T(8,128)(2,1)S(1)} %get-tuple-element.35.refs_1_.refs_0_, bf16[128,2048]{1,0:T(8,128)(2,1)S(1)} %get-tuple-element.36.refs_2_.refs_1_, ...), custom_call_target="tpu_custom_call" | custom-call | flops 10000000000 | bytes 8388608 | tf_op jit(solution)/shard_map/inner/pallas_call | solution.py:503
  18.8 1.2 %collective-permute-done.3.refs_1_ = f32[4,32,128]{2,1,0:T(8,128)S(1)} collective-permute-done((f32[4,32,128]{2,1,0:T(8,128)S(1)}, f32[4,32,128]{2,1,0:T(8,128)S(1)}, u32[]{:S(2)}, u32[]{:S(2)}) %collective-permute-start.3) | collective-permute-done | bytes 65568 | tf_op jit(solution)/shard_map/ppermute | solution.py:582
  20.0 1.6 %collective-permute-start.4 = (f32[2,32,128]{2,1,0:T(8,128)S(1)}, f32[2,32,128]{2,1,0:T(8,128)S(1)}, u32[]{:S(2)}, u32[]{:S(2)}) collective-permute-start(f32[2,32,128]{2,1,0:T(8,128)S(1)} %get-tuple-element.63), channel_id=1, source_target_pairs={{0,4},{1,5},{2,6},{3,7},{4,0},{5,1},{6,2},{7,3},{8,12},{9,13},{10,... | collective-permute-start | bytes 98312 | tf_op jit(solution)/shard_map/ppermute | solution.py:582
  21.7 4.8 %inner.2 = (f32[128,1536]{1,0:T(8,128)S(1)}, f32[128,1536]{1,0:T(8,128)S(1)}, f32[128,1536]{1,0:T(8,128)S(1)}) custom-call(bf16[128,2048]{1,0:T(8,128)(2,1)S(1)} %get-tuple-element.45.refs_0_, bf16[128,2048]{1,0:T(8,128)(2,1)S(1)} %get-tuple-element.35.refs_1_.refs_0_, bf16[128,2048]{1,0:T(8,128)(2,1)S(1)} %get-tuple-element.36.refs_2_.refs_1_, ...), custom_call_target="tpu_custom_call" | custom-call | flops 10000000000 | bytes 8388608 | tf_op jit(solution)/shard_map/inner/pallas_call | solution.py:503
  26.5 0.0 collective-permute-done.4.refs_1_
  26.5 2.6 %collective-permute-start.5 = (f32[1,32,128]{2,1,0:T(8,128)S(1)}, f32[1,32,128]{2,1,0:T(8,128)S(1)}, u32[]{:S(2)}, u32[]{:S(2)}) collective-permute-start(f32[1,32,128]{2,1,0:T(8,128)S(1)} %get-tuple-element.65), channel_id=1, source_target_pairs={{0,8},{1,9},{2,10},{3,11},{4,12},{5,13},{6,14},{7,15},{8,0},{9,1},... | collective-permute-start | bytes 49160 | tf_op jit(solution)/shard_map/ppermute | solution.py:582
  29.2 1.2 %shard_map.102 = (bf16[128,2048]{1,0:T(8,128)(2,1)}, bf16[128,2048]{1,0:T(8,128)(2,1)}, bf16[128,2048]{1,0:T(8,128)(2,1)}) custom-call(bf16[128,2048]{1,0:T(8,128)(2,1)S(1)} %get-tuple-element.37.refs_4_.refs_0_.refs_2_, f32[64,2048]{1,0:T(8,128)S(1)} %get-tuple-element.39.refs_3_.refs_1_, f32[128,2048]{1,0:T(8,128)S(1)} %get-tuple-element.43.refs_2_.refs_4_, ...), custom_call_target="tpu_custom_call" | custom-call | flops 3000000000 | bytes 9437184 | tf_op jit(solution)/shard_map/pallas_call | solution.py:532
  30.3 0.9 %collective-permute-done.5 = f32[1,32,128]{2,1,0:T(8,128)S(1)} collective-permute-done((f32[1,32,128]{2,1,0:T(8,128)S(1)}, f32[1,32,128]{2,1,0:T(8,128)S(1)}, u32[]{:S(2)}, u32[]{:S(2)}) %collective-permute-start.5) | collective-permute-done | bytes 16416 | tf_op jit(solution)/shard_map/ppermute | solution.py:582
  31.3 0.6 %add_bitcast_fusion = f32[128,32]{0,1:T(8,128)} fusion(f32[1,32,128]{2,1,0:T(8,128)S(1)} %get-tuple-element.64, f32[1,32,128]{2,1,0:T(8,128)S(1)} %collective-permute-done.5), kind=kLoop, calls=%fused_computation | loop fusion | flops 4096 | bytes 49152 | tf_op jit(solution)/shard_map/reshape | solution.py:588
  31.9 0.0 collective-permute-done.refs_3_
  31.9 1.7 %shard_map.103 = (bf16[128,2048]{1,0:T(8,128)(2,1)}, bf16[128,2048]{1,0:T(8,128)(2,1)}, bf16[128,2048]{1,0:T(8,128)(2,1)}) custom-call(bf16[128,2048]{1,0:T(8,128)(2,1)S(1)} %get-tuple-element.35.refs_1_.refs_0_, bf16[128,2048]{1,0:T(8,128)(2,1)S(1)} %get-tuple-element.36.refs_2_.refs_1_, ...), custom_call_target="tpu_custom_call", output_to_operand_aliasing={{0}: (12, {}), {1}: (13, {}), {2}: (14, {})} | custom-call | flops 3000000000 | bytes 9437184 | tf_op jit(solution)/shard_map/pallas_call | solution.py:532
  (4 shorter events, 0.1 us)
Async XLA Ops:
  3.0 9.7 %collective-permute-start.1 = (f32[17,32,128]{2,1,0:T(8,128)S(1)}, f32[17,32,128]{2,1,0:T(8,128)S(1)}, u32[]{:S(2)}, u32[]{:S(2)}) collective-permute-start(f32[17,32,128]{2,1,0:T(8,128)S(1)} %get-tuple-element.40.refs_4_.refs_0_), channel_id=1, source_target_pairs={{0,16},{16,0},{1,17},{17,1},{2,18},{18,2},{3,19},{19,3},{4,20},{20... | collective-permute-start | bytes 835592 | tf_op jit(solution)/shard_map/ppermute | solution.py:573
  12.7 2.9 %collective-permute-start.2 = (f32[8,32,128]{2,1,0:T(8,128)S(1)}, f32[8,32,128]{2,1,0:T(8,128)S(1)}, u32[]{:S(2)}, u32[]{:S(2)}) collective-permute-start(f32[8,32,128]{2,1,0:T(8,128)S(1)} %get-tuple-element.59), channel_id=1, source_target_pairs={{0,1},{1,0},{2,3},{3,2},{4,5},{5,4},{6,7},{7,6},{8,9},{9,8},{10,11... | collective-permute-start | bytes 393224 | tf_op jit(solution)/shard_map/ppermute | solution.py:582
  13.8 18.1 %collective-permute-start = (f32[16,64,128]{2,1,0:T(8,128)S(1)}, f32[16,64,128]{2,1,0:T(8,128)S(1)}, u32[]{:S(2)}, u32[]{:S(2)}) collective-permute-start(f32[16,64,128]{2,1,0:T(8,128)S(1)} %get-tuple-element.42), channel_id=1, source_target_pairs={{0,16},{16,0},{1,17},{17,1},{2,18},{18,2},{3,19},{19,3},{4,20},{20... | collective-permute-start | bytes 1572872 | tf_op jit(solution)/shard_map/ppermute | solution.py:575
  15.6 1.6 %copy-start = (f32[32,64]{1,0:T(8,128)S(1)}, f32[32,64]{1,0:T(8,128)}, u32[]{:S(2)}) copy-start(f32[32,64]{1,0:T(8,128)} %refs_5_.3) | copy-start | bytes 24580
  15.7 4.3 %collective-permute-start.3 = (f32[4,32,128]{2,1,0:T(8,128)S(1)}, f32[4,32,128]{2,1,0:T(8,128)S(1)}, u32[]{:S(2)}, u32[]{:S(2)}) collective-permute-start(f32[4,32,128]{2,1,0:T(8,128)S(1)} %get-tuple-element.61), channel_id=1, source_target_pairs={{0,2},{1,3},{2,0},{3,1},{4,6},{5,7},{6,4},{7,5},{8,10},{9,11},{10,... | collective-permute-start | bytes 196616 | tf_op jit(solution)/shard_map/ppermute | solution.py:582
  20.0 6.5 %collective-permute-start.4 = (f32[2,32,128]{2,1,0:T(8,128)S(1)}, f32[2,32,128]{2,1,0:T(8,128)S(1)}, u32[]{:S(2)}, u32[]{:S(2)}) collective-permute-start(f32[2,32,128]{2,1,0:T(8,128)S(1)} %get-tuple-element.63), channel_id=1, source_target_pairs={{0,4},{1,5},{2,6},{3,7},{4,0},{5,1},{6,2},{7,3},{8,12},{9,13},{10,... | collective-permute-start | bytes 98312 | tf_op jit(solution)/shard_map/ppermute | solution.py:582
  26.5 4.7 %collective-permute-start.5 = (f32[1,32,128]{2,1,0:T(8,128)S(1)}, f32[1,32,128]{2,1,0:T(8,128)S(1)}, u32[]{:S(2)}, u32[]{:S(2)}) collective-permute-start(f32[1,32,128]{2,1,0:T(8,128)S(1)} %get-tuple-element.65), channel_id=1, source_target_pairs={{0,8},{1,9},{2,10},{3,11},{4,12},{5,13},{6,14},{7,15},{8,0},{9,1},... | collective-permute-start | bytes 49160 | tf_op jit(solution)/shard_map/ppermute | solution.py:582

commit v4 on v3

--- a/solution.py
+++ b/solution.py
@@ -120,9 +120,10 @@
         if fast:
             sent, kept = outs
             half = grad.shape[0] // 2
-            sent[pair] = jnp.where(is_first, grad[half:], grad[:half])
+            sent[pair * half : (pair + 1) * half] = jnp.where(is_first, grad[half:], grad[:half])
             kept[pair] = jnp.where(is_first, grad[:half], grad[half:])
-            sent[sent.shape[0] - 1, pair : pair + 1] = whole
+            row = kept.shape[0] * half + pair
+            sent[row : row + 1] = whole
         else:
             grads, wholes = outs
             grads[pair] = grad
@@ -157,7 +158,8 @@
         state = diagonal(state[:, :LANES] + state[:, LANES:])
         if fast:
             sent, kept = refs[:2]
-            grad = jnp.concatenate([sent[pair], kept[pair]], 0)
+            half = kept.shape[1]
+            grad = jnp.concatenate([sent[pair * half : (pair + 1) * half], kept[pair]], 0)
             state_out[pair] = jnp.where(is_first, whole * init[:, at] + state, grad)
         else:
             state_out[pair] = state
@@ -224,7 +226,7 @@
         for c in range(chunks):
             here = rows[c]
             count = (c + 1) * CHUNK
-            pieces = [key_late[here] * jnp.exp(middles[c] - totals[c])]
+            pieces = [kf[here] * (late[here] * jnp.exp(middles[c] - totals[c]))]
             gap = middles[c]
             for e in reversed(range(c)):
                 pieces.append(key_late[rows[e]] * jnp.exp(gap))
@@ -238,7 +240,7 @@
             got = got[: 2 * CHUNK] + got[2 * CHUNK :]
             got = jnp.where(keep_chunk, got[:CHUNK], got[CHUNK:])
             rec_rows.append(early[here] * jnp.exp(-middles[c]) * got)
-            pieces = [rec_early[here] * jnp.exp(-middles[c])]
+            pieces = [rf[here] * (early[here] * jnp.exp(-middles[c]))]
             gap = totals[c] - middles[c]
             for e in range(c + 1, chunks):
                 pieces.append(rec_early[rows[e]] * jnp.exp(gap))
@@ -414,12 +416,13 @@
 def share_kernel(blocks, sent, kept, got, mine, theirs):
     is_first = lax.axis_index("seq") == 0
     upper = lax.axis_index("dp") & 1
-    last = sent.shape[0] - 1
+    half = kept.shape[1]
     for b in range(blocks // 2):
         for ref, low in ((mine, upper), (theirs, 1 - upper)):
             p = 2 * b + low
-            whole = jnp.where(is_first, sent[last, pl.ds(p, 1), :], got[last, pl.ds(p, 1), :])
-            own, other = kept[p], got[p]
+            row = pl.ds(blocks * half + p, 1)
+            whole = jnp.where(is_first, sent[row], got[row])
+            own, other = kept[p], got[pl.ds(pl.multiple_of(p * half, half), half)]
             ref[b] = jnp.where(is_first, own, other) + whole * jnp.where(is_first, other, own)
 
 
@@ -442,7 +445,7 @@
         and seq_size == 2
         and dp_size & (dp_size - 1) == 0
         and pairs == dp_size
-        and pairs <= half
+        and pairs % 8 == 0
     )
     seq = lax.axis_index("seq")
     is_first = seq == 0
@@ -462,7 +465,7 @@
 
     def grads(b):
         if fast:
-            shapes = (like((pairs + 1, half, LANES)), like((pairs, half, LANES)))
+            shapes = (like((pairs * (half + 1), LANES)), like((pairs, half, LANES)))
         else:
             shapes = (like((pairs, feature, LANES)), like((pairs, 1, LANES)))
         operands = (f[b], r[b], dy[b], k[b], v[b], init_t)

time: 33.8 us -> 33.7 us (level)
  no operation moved by 1% of the time
where the time goes in v4:
time: 33.7 us; the launch traced here: 33.5 us
  Pallas kernels  12.7 us (38%)
  starting transfers between devices  10.8 us (32%)
  waiting for transfers between devices  8.61 us (26%)
  between operations  0.71 us (2%)
  other arithmetic  0.61 us (2%)
    ppermute x1, waiting for transfers between devices, on_device(): got = lax.ppermute(sent, 'seq', swap)  6.48 us
    pallas_call x2, Pallas kernels, inner(): pl.pallas_call(body, in_specs=[vmem] * 6, out_specs=(vmem,) * 3, out_shap...  6.39 us
    ppermute x4, starting transfers between devices, on_device(): got = lax.ppermute(theirs, 'dp', [(i, i ^ bit) for i in range(dp_size)])  5.95 us
    ppermute x1, starting transfers between devices, on_device(): got = lax.ppermute(sent, 'seq', swap)  3.03 us
    pallas_call x2, Pallas kernels, finish(): pl.pallas_call(lambda *refs: kernel(group, *refs[:count], *refs[count + l...  2.87 us
    pallas_call x1, Pallas kernels, grads(): pl.pallas_call(lambda *refs: grad_kernel(state_group, fast, *refs), in_sp...  2.33 us
    ppermute x4, waiting for transfers between devices, on_device(): got = lax.ppermute(theirs, 'dp', [(i, i ^ bit) for i in range(dp_size)])  2.13 us
    ppermute x1, starting transfers between devices, on_device(): other = lax.ppermute(swapped, 'seq', swap)  1.81 us
  transfers between devices with their start and end apart: 6, of which 3 were waited for; matrix products, arithmetic and copies ran while one was open for 2% of the time, Pallas kernels for 26%

profile of v4, /device:TPU:0, one launch (start us, length us, event | category | flops | bytes accessed | tf_op | source)
XLA Modules:
  0.0 33.5 jit_solution(10917070994282803640)
XLA Ops:
  0.6 2.3 %grads.1 = (bf16[128,2048]{1,0:T(8,128)(2,1)S(1)}, bf16[128,2048]{1,0:T(8,128)(2,1)S(1)}, bf16[128,2048]{1,0:T(8,128)(2,1)S(1)}, bf16[128,2048]{1,0:T(8,128)(2,1...) custom-call(bf16[128,2048]{1,0:T(8,128)(2,1)} %bitcast.13, ...), custom_call_target="tpu_custom_call" | custom-call | flops 4000000000 | bytes 4194304 | tf_op jit(solution)/shard_map/grads/pallas_call | solution.py:472
  3.0 3.0 %collective-permute-start.1 = (f32[528,128]{1,0:T(8,128)S(1)}, f32[528,128]{1,0:T(8,128)S(1)}, u32[]{:S(2)}, u32[]{:S(2)}) collective-permute-start(f32[528,128]{1,0:T(8,128)S(1)} %get-tuple-element.40.refs_4_.refs_0_), channel_id=1, source_target_pairs={{0,16},{16,0},{1,17},{17,1},{2,18},{18,2},{3,19},{19,3},{4,20},{20... | collective-permute-start | bytes 811016 | tf_op jit(solution)/shard_map/ppermute | solution.py:576
  6.0 6.5 %collective-permute-done.1.refs_2_ = f32[528,128]{1,0:T(8,128)S(1)} collective-permute-done((f32[528,128]{1,0:T(8,128)S(1)}, f32[528,128]{1,0:T(8,128)S(1)}, u32[]{:S(2)}, u32[]{:S(2)}) %collective-permute-start.1) | collective-permute-done | bytes 270368 | tf_op jit(solution)/shard_map/ppermute | solution.py:576
  12.5 0.1 share.1
  12.5 0.1 collective-permute-start.2
  12.6 1.0 %ends.1 = (f32[128,2048]{1,0:T(8,128)S(1)}, f32[16,64,128]{2,1,0:T(8,128)S(1)}) custom-call(bf16[128,2048]{1,0:T(8,128)(2,1)S(1)} %get-tuple-element.38.refs_0_.refs_3_, bf16[128,2048]{1,0:T(8,128)(2,1)S(1)} %get-tuple-element.35.refs_1_.refs_0_, bf16[128,2048]{1,0:T(8,128)(2,1)S(1)} %get-tuple-element.36.refs_2_.refs_1_, ...), custom_call_target="tpu_custom_call" | custom-call | flops 4000000000 | bytes 4194304 | tf_op jit(solution)/shard_map/ends/pallas_call | solution.py:490
  13.7 1.8 %collective-permute-start = (f32[16,64,128]{2,1,0:T(8,128)S(1)}, f32[16,64,128]{2,1,0:T(8,128)S(1)}, u32[]{:S(2)}, u32[]{:S(2)}) collective-permute-start(f32[16,64,128]{2,1,0:T(8,128)S(1)} %get-tuple-element.42), channel_id=1, source_target_pairs={{0,16},{16,0},{1,17},{17,1},{2,18},{18,2},{3,19},{19,3},{4,20},{20... | collective-permute-start | bytes 1572872 | tf_op jit(solution)/shard_map/ppermute | solution.py:578
  15.5 0.0 collective-permute-done.2.refs_1_
  15.5 0.0 copy-start
  15.5 1.6 %collective-permute-start.3 = (f32[4,32,128]{2,1,0:T(8,128)S(1)}, f32[4,32,128]{2,1,0:T(8,128)S(1)}, u32[]{:S(2)}, u32[]{:S(2)}) collective-permute-start(f32[4,32,128]{2,1,0:T(8,128)S(1)} %get-tuple-element.61), channel_id=1, source_target_pairs={{0,2},{1,3},{2,0},{3,1},{4,6},{5,7},{6,4},{7,5},{8,10},{9,11},{10,... | collective-permute-start | bytes 196616 | tf_op jit(solution)/shard_map/ppermute | solution.py:585
  17.1 0.0 copy-done
  17.1 1.5 %inner.3 = (f32[128,512]{1,0:T(8,128)S(1)}, f32[128,512]{1,0:T(8,128)S(1)}, f32[128,512]{1,0:T(8,128)S(1)}) custom-call(bf16[128,2048]{1,0:T(8,128)(2,1)S(1)} %get-tuple-element.45.refs_0_, bf16[128,2048]{1,0:T(8,128)(2,1)S(1)} %get-tuple-element.35.refs_1_.refs_0_, bf16[128,2048]{1,0:T(8,128)(2,1)S(1)} %get-tuple-element.36.refs_2_.refs_1_, ...), custom_call_target="tpu_custom_call" | custom-call | flops 10000000000 | bytes 8388608 | tf_op jit(solution)/shard_map/inner/pallas_call | solution.py:506
  18.7 1.2 %collective-permute-done.3.refs_1_ = f32[4,32,128]{2,1,0:T(8,128)S(1)} collective-permute-done((f32[4,32,128]{2,1,0:T(8,128)S(1)}, f32[4,32,128]{2,1,0:T(8,128)S(1)}, u32[]{:S(2)}, u32[]{:S(2)}) %collective-permute-start.3) | collective-permute-done | bytes 65568 | tf_op jit(solution)/shard_map/ppermute | solution.py:585
  19.9 1.6 %collective-permute-start.4 = (f32[2,32,128]{2,1,0:T(8,128)S(1)}, f32[2,32,128]{2,1,0:T(8,128)S(1)}, u32[]{:S(2)}, u32[]{:S(2)}) collective-permute-start(f32[2,32,128]{2,1,0:T(8,128)S(1)} %get-tuple-element.63), channel_id=1, source_target_pairs={{0,4},{1,5},{2,6},{3,7},{4,0},{5,1},{6,2},{7,3},{8,12},{9,13},{10,... | collective-permute-start | bytes 98312 | tf_op jit(solution)/shard_map/ppermute | solution.py:585
  21.5 4.8 %inner.2 = (f32[128,1536]{1,0:T(8,128)S(1)}, f32[128,1536]{1,0:T(8,128)S(1)}, f32[128,1536]{1,0:T(8,128)S(1)}) custom-call(bf16[128,2048]{1,0:T(8,128)(2,1)S(1)} %get-tuple-element.45.refs_0_, bf16[128,2048]{1,0:T(8,128)(2,1)S(1)} %get-tuple-element.35.refs_1_.refs_0_, bf16[128,2048]{1,0:T(8,128)(2,1)S(1)} %get-tuple-element.36.refs_2_.refs_1_, ...), custom_call_target="tpu_custom_call" | custom-call | flops 10000000000 | bytes 8388608 | tf_op jit(solution)/shard_map/inner/pallas_call | solution.py:506
  26.3 0.0 collective-permute-done.4.refs_1_
  26.4 2.7 %collective-permute-start.5 = (f32[1,32,128]{2,1,0:T(8,128)S(1)}, f32[1,32,128]{2,1,0:T(8,128)S(1)}, u32[]{:S(2)}, u32[]{:S(2)}) collective-permute-start(f32[1,32,128]{2,1,0:T(8,128)S(1)} %get-tuple-element.65), channel_id=1, source_target_pairs={{0,8},{1,9},{2,10},{3,11},{4,12},{5,13},{6,14},{7,15},{8,0},{9,1},... | collective-permute-start | bytes 49160 | tf_op jit(solution)/shard_map/ppermute | solution.py:585
  29.0 1.2 %shard_map.102 = (bf16[128,2048]{1,0:T(8,128)(2,1)}, bf16[128,2048]{1,0:T(8,128)(2,1)}, bf16[128,2048]{1,0:T(8,128)(2,1)}) custom-call(bf16[128,2048]{1,0:T(8,128)(2,1)S(1)} %get-tuple-element.37.refs_4_.refs_0_.refs_2_, f32[64,2048]{1,0:T(8,128)S(1)} %get-tuple-element.39.refs_3_.refs_1_, f32[128,2048]{1,0:T(8,128)S(1)} %get-tuple-element.43.refs_2_.refs_4_, ...), custom_call_target="tpu_custom_call" | custom-call | flops 3000000000 | bytes 9437184 | tf_op jit(solution)/shard_map/pallas_call | solution.py:535
  30.2 0.9 %collective-permute-done.5 = f32[1,32,128]{2,1,0:T(8,128)S(1)} collective-permute-done((f32[1,32,128]{2,1,0:T(8,128)S(1)}, f32[1,32,128]{2,1,0:T(8,128)S(1)}, u32[]{:S(2)}, u32[]{:S(2)}) %collective-permute-start.5) | collective-permute-done | bytes 16416 | tf_op jit(solution)/shard_map/ppermute | solution.py:585
  31.2 0.6 %add_bitcast_fusion = f32[128,32]{0,1:T(8,128)} fusion(f32[1,32,128]{2,1,0:T(8,128)S(1)} %get-tuple-element.64, f32[1,32,128]{2,1,0:T(8,128)S(1)} %collective-permute-done.5), kind=kLoop, calls=%fused_computation | loop fusion | flops 4096 | bytes 49152 | tf_op jit(solution)/shard_map/reshape | solution.py:591
  31.8 0.0 collective-permute-done.refs_3_
  31.8 1.7 %shard_map.103 = (bf16[128,2048]{1,0:T(8,128)(2,1)}, bf16[128,2048]{1,0:T(8,128)(2,1)}, bf16[128,2048]{1,0:T(8,128)(2,1)}) custom-call(bf16[128,2048]{1,0:T(8,128)(2,1)S(1)} %get-tuple-element.35.refs_1_.refs_0_, bf16[128,2048]{1,0:T(8,128)(2,1)S(1)} %get-tuple-element.36.refs_2_.refs_1_, ...), custom_call_target="tpu_custom_call", output_to_operand_aliasing={{0}: (12, {}), {1}: (13, {}), {2}: (14, {})} | custom-call | flops 3000000000 | bytes 9437184 | tf_op jit(solution)/shard_map/pallas_call | solution.py:535
  (3 shorter events, 0.0 us)
Async XLA Ops:
  3.0 9.5 %collective-permute-start.1 = (f32[528,128]{1,0:T(8,128)S(1)}, f32[528,128]{1,0:T(8,128)S(1)}, u32[]{:S(2)}, u32[]{:S(2)}) collective-permute-start(f32[528,128]{1,0:T(8,128)S(1)} %get-tuple-element.40.refs_4_.refs_0_), channel_id=1, source_target_pairs={{0,16},{16,0},{1,17},{17,1},{2,18},{18,2},{3,19},{19,3},{4,20},{20... | collective-permute-start | bytes 811016 | tf_op jit(solution)/shard_map/ppermute | solution.py:576
  12.5 2.9 %collective-permute-start.2 = (f32[8,32,128]{2,1,0:T(8,128)S(1)}, f32[8,32,128]{2,1,0:T(8,128)S(1)}, u32[]{:S(2)}, u32[]{:S(2)}) collective-permute-start(f32[8,32,128]{2,1,0:T(8,128)S(1)} %get-tuple-element.59), channel_id=1, source_target_pairs={{0,1},{1,0},{2,3},{3,2},{4,5},{5,4},{6,7},{7,6},{8,9},{9,8},{10,11... | collective-permute-start | bytes 393224 | tf_op jit(solution)/shard_map/ppermute | solution.py:585
  13.7 18.1 %collective-permute-start = (f32[16,64,128]{2,1,0:T(8,128)S(1)}, f32[16,64,128]{2,1,0:T(8,128)S(1)}, u32[]{:S(2)}, u32[]{:S(2)}) collective-permute-start(f32[16,64,128]{2,1,0:T(8,128)S(1)} %get-tuple-element.42), channel_id=1, source_target_pairs={{0,16},{16,0},{1,17},{17,1},{2,18},{18,2},{3,19},{19,3},{4,20},{20... | collective-permute-start | bytes 1572872 | tf_op jit(solution)/shard_map/ppermute | solution.py:578
  15.5 1.6 %copy-start = (f32[32,64]{1,0:T(8,128)S(1)}, f32[32,64]{1,0:T(8,128)}, u32[]{:S(2)}) copy-start(f32[32,64]{1,0:T(8,128)} %refs_5_.3) | copy-start | bytes 24580
  15.5 4.3 %collective-permute-start.3 = (f32[4,32,128]{2,1,0:T(8,128)S(1)}, f32[4,32,128]{2,1,0:T(8,128)S(1)}, u32[]{:S(2)}, u32[]{:S(2)}) collective-permute-start(f32[4,32,128]{2,1,0:T(8,128)S(1)} %get-tuple-element.61), channel_id=1, source_target_pairs={{0,2},{1,3},{2,0},{3,1},{4,6},{5,7},{6,4},{7,5},{8,10},{9,11},{10,... | collective-permute-start | bytes 196616 | tf_op jit(solution)/shard_map/ppermute | solution.py:585
  19.9 6.5 %collective-permute-start.4 = (f32[2,32,128]{2,1,0:T(8,128)S(1)}, f32[2,32,128]{2,1,0:T(8,128)S(1)}, u32[]{:S(2)}, u32[]{:S(2)}) collective-permute-start(f32[2,32,128]{2,1,0:T(8,128)S(1)} %get-tuple-element.63), channel_id=1, source_target_pairs={{0,4},{1,5},{2,6},{3,7},{4,0},{5,1},{6,2},{7,3},{8,12},{9,13},{10,... | collective-permute-start | bytes 98312 | tf_op jit(solution)/shard_map/ppermute | solution.py:585
  26.4 4.8 %collective-permute-start.5 = (f32[1,32,128]{2,1,0:T(8,128)S(1)}, f32[1,32,128]{2,1,0:T(8,128)S(1)}, u32[]{:S(2)}, u32[]{:S(2)}) collective-permute-start(f32[1,32,128]{2,1,0:T(8,128)S(1)} %get-tuple-element.65), channel_id=1, source_target_pairs={{0,8},{1,9},{2,10},{3,11},{4,12},{5,13},{6,14},{7,15},{8,0},{9,1},... | collective-permute-start | bytes 49160 | tf_op jit(solution)/shard_map/ppermute | solution.py:585
